TPU v7x, 256 devices: a whole 4x4x8 slice. The times are simulated.
256 devices in a mesh: batch: 8 (over z), rows: 32 (over y, x, core).
Axes of the slice: x: 4, y: 4, z: 8, core: 2. Of those that a mesh axis runs over, the one named last changes fastest.
Arguments:
- level_two: bfloat16 [16, 256, 256, 256], P('batch', 'rows'), parts along dimension 0, may hold values from -130 to 130
- level_three: bfloat16 [16, 128, 128, 512], P('batch', 'rows'), parts along dimension 0, may hold values from -130 to 130
- level_four: bfloat16 [16, 64, 64, 1024], P('batch', 'rows'), parts along dimension 0, may hold values from -130 to 130
- level_five: bfloat16 [16, 32, 32, 2048], P('batch', 'rows'), parts along dimension 0, may hold values from -130 to 130
- lateral_two: bfloat16 [256, 256], replicated, may hold values from -0.375 to 0.375
- lateral_three: bfloat16 [512, 256], replicated, may hold values from -0.25 to 0.25
- lateral_four: bfloat16 [1024, 256], replicated, may hold values from -0.1875 to 0.1875
- lateral_five: bfloat16 [2048, 256], replicated, may hold values from -0.125 to 0.125
- lateral_bias: float32 [4, 256], replicated, may hold values from -4 to 4
- smooth_weight: bfloat16 [4, 3, 768, 256], replicated, may hold values from -0.125 to 0.125
- norm_gain: float32 [4, 256], replicated, may hold values from 0.5 to 1.5
- norm_shift: float32 [4, 256], replicated, may hold values from -2 to 2
Outputs:
- pyramid_two: bfloat16 [16, 256, 256, 256], P('batch', 'rows'), parts along dimension 0
- pyramid_three: bfloat16 [16, 128, 128, 256], P('batch', 'rows'), parts along dimension 0
- pyramid_four: bfloat16 [16, 64, 64, 256], P('batch', 'rows'), parts along dimension 0
- pyramid_five: bfloat16 [16, 32, 32, 256], P('batch', 'rows'), parts along dimension 0
There are 8 independent parts, one for each index of `batch`. A program takes and returns all parts, laid end to end along the dimension named above; an argument that names none is the same for every part. Nothing has to cross between parts.
All inputs are finite; a program needn't handle non-finite values.
Results may differ from a plain program's by a relative error of at most 0.0054.
Values may be sent and summed in bfloat16 or wider, within the bound.
A program may use at most 128 MiB of HBM per device.

v0:
```python
import functools

import jax
import jax.numpy as jnp
from jax import lax
from jax.sharding import Mesh
from jax.sharding import PartitionSpec as P

GROUPS = 32
ROWS = ("rows_0", "rows_1", "rows_2")


epsilon = 1e-05


def with_halo(cells, sides, width):
    for axis, dim in sides:
        count = lax.axis_size(axis)
        ends = count - 1
        head = lax.slice_in_dim(cells, 0, width, axis=dim)
        tail = lax.slice_in_dim(cells, cells.shape[dim] - width, cells.shape[dim], axis=dim)
        cells = jnp.concatenate(
            [
                lax.ppermute(tail, axis, [(i, (i + 1) % count) for i in range(ends)]),
                cells,
                lax.ppermute(head, axis, [((i + 1) % count, i) for i in range(ends)]),
            ],
            axis=dim,
        )
    return cells


def one_axis_at_a_time(shard, axes):
    return functools.reduce(lax.psum, axes, shard)


def refine(widened, axis_pos):
    length = widened.shape[axis_pos] - 2
    before = lax.slice_in_dim(widened, 0, length, axis=axis_pos)
    middle = lax.slice_in_dim(widened, 1, length + 1, axis=axis_pos)
    beyond = lax.slice_in_dim(widened, 2, length + 2, axis=axis_pos)
    even_rows = 0.25 * before + 0.75 * middle
    odd_rows = 0.75 * middle + 0.25 * beyond
    stacked = jnp.stack([even_rows, odd_rows], axis_pos + 1)
    new_shape = list(widened.shape)
    new_shape[axis_pos] = 2 * length
    return stacked.reshape(new_shape)


def edge_columns(values):
    return jnp.concatenate([values[:, :, :1], values, values[:, :, -1:]], 2)


def edge_rows_clamp(widened, position, strips):
    first_row = jnp.where(position == 0, widened[:, 1:2], widened[:, 0:1])
    last_row = jnp.where(position == strips - 1, widened[:, -2:-1], widened[:, -1:])
    return jnp.concatenate([first_row, widened[:, 1:-1], last_row], 1)


def lateral(feature, weight, bias_row):
    flattened = feature.reshape(-1, feature.shape[-1])
    result = jnp.dot(flattened, weight, preferred_element_type=jnp.float32) + bias_row
    return result.reshape(feature.shape[:-1] + (weight.shape[1],))


def conv_three(widened, weight):
    padded = jnp.pad(widened, ((0, 0), (0, 0), (1, 1), (0, 0)))
    strip_rows = widened.shape[1] - 2
    width_cells = widened.shape[2]
    channels = widened.shape[3]
    result = jnp.zeros((widened.shape[0] * strip_rows * width_cells, weight.shape[2]), jnp.float32)
    for tap_row in range(3):
        band_rows = padded[:, tap_row : tap_row + strip_rows]
        stacked = jnp.concatenate(
            [
                band_rows[:, :, 0:width_cells],
                band_rows[:, :, 1 : width_cells + 1],
                band_rows[:, :, 2 : width_cells + 2],
            ],
            3,
        )
        result = result + jnp.dot(
            stacked.reshape(-1, 3 * channels), weight[tap_row], preferred_element_type=jnp.float32
        )
    return result.reshape(widened.shape[0], strip_rows, width_cells, weight.shape[2])


def group_sums(conv_out):
    dims_all = conv_out.shape
    grouped = conv_out.reshape(dims_all[0], -1, GROUPS, dims_all[3] // GROUPS)
    return (jnp.sum(grouped, axis=(1, 3)), jnp.sum(grouped * grouped, axis=(1, 3)))


def normalize(conv_out, totals, squares, entries, gain_row, shift_row):
    mean_val = totals / entries
    variance = squares / entries - mean_val * mean_val
    scale_inv = lax.rsqrt(variance + epsilon)
    dims_all = conv_out.shape
    grouped = conv_out.reshape(dims_all[0], dims_all[1], dims_all[2], GROUPS, dims_all[3] // GROUPS)
    centred = (grouped - mean_val[:, None, None, :, None]) * scale_inv[:, None, None, :, None]
    return (centred.reshape(dims_all) * gain_row + shift_row).astype(jnp.bfloat16)


def per_device(
    level_two,
    level_three,
    level_four,
    level_five,
    lateral_two,
    lateral_three,
    lateral_four,
    lateral_five,
    lateral_bias,
    smooth_weight,
    norm_gain,
    norm_shift,
):
    position = lax.axis_index(ROWS)
    strips = lax.axis_size(ROWS)
    features = (level_two, level_three, level_four, level_five)
    weights = (lateral_two, lateral_three, lateral_four, lateral_five)
    widened_in = [None, None, None, None]
    laterals = [
        lateral(features[level_idx], weights[level_idx], lateral_bias[level_idx])
        for level_idx in range(4)
    ]
    merged = laterals[3].astype(jnp.bfloat16)
    for level_idx in (3, 2, 1, 0):
        if level_idx < 3:
            coarse = edge_rows_clamp(widened_in[level_idx + 1], position, strips).astype(
                jnp.float32
            )
            upsampled = refine(edge_columns(refine(coarse, 1)), 2)
            merged = (laterals[level_idx] + upsampled).astype(jnp.bfloat16)
        widened_in[level_idx] = with_halo(merged, ((ROWS, 1),), 1)
    results = []
    for level_idx in range(4):
        conv_out = conv_three(widened_in[level_idx], smooth_weight[level_idx])
        totals, squares = group_sums(conv_out)
        totals, squares = (one_axis_at_a_time(totals, ROWS), one_axis_at_a_time(squares, ROWS))
        entries = float(
            conv_out.shape[1] * strips * conv_out.shape[2] * (conv_out.shape[3] // GROUPS)
        )
        results.append(
            normalize(
                conv_out, totals, squares, entries, norm_gain[level_idx], norm_shift[level_idx]
            )
        )
    return (results[0], results[1], results[2], results[3])


def solution(mesh):
    torus = Mesh(
        mesh.devices.reshape(mesh.shape["batch"], 4, 4, 2), ("batch", "rows_0", "rows_1", "rows_2")
    )
    in_specs = (
        P("batch", ROWS, None, None),
        P("batch", ROWS, None, None),
        P("batch", ROWS, None, None),
        P("batch", ROWS, None, None),
        P(),
        P(),
        P(),
        P(),
        P(),
        P(),
        P(),
        P(),
    )
    out_specs = (
        P("batch", ROWS, None, None),
        P("batch", ROWS, None, None),
        P("batch", ROWS, None, None),
        P("batch", ROWS, None, None),
    )
    return jax.shard_map(
        per_device, mesh=torus, in_specs=in_specs, out_specs=out_specs, check_vma=False
    )
```

profile of v0, /device:TPU:1, one launch (start us, length us, event | category | flops | bytes accessed | tf_op | source)
XLA Modules:
  0.0 185.7 jit_solution(9364880712879425566)
XLA Ops:
  1.6 1.6 fusion.23
  3.2 5.1 %collective-permute-start.1 = (bf16[2,1,32,256]{3,2,0,1:T(8,128)(2,1)S(1)}, bf16[2,1,32,256]{3,2,0,1:T(8,128)(2,1)S(1)}, u32[]{:S(2)}, u32[]{:S(2)}) collective-permute-start(bf16[2,1,32,256]{3,2,0,1:T(8,128)(2,1)S(1)} %bitcast.161), channel_id=1, source_target_pairs={{1,0},{2,1},{3,2},{4,3},{5,4},{6,5},{7,6},{8,7},{9,8},{10,9},{11,1... | collective-permute-start | bytes 98312 | tf_op jit(solution)/shard_map/ppermute | solution.py:26
  8.3 1.9 %collective-permute-start = (bf16[2,1,32,256]{3,2,0,1:T(8,128)(2,1)S(1)}, bf16[2,1,32,256]{3,2,0,1:T(8,128)(2,1)S(1)}, u32[]{:S(2)}, u32[]{:S(2)}) collective-permute-start(bf16[2,1,32,256]{3,2,0,1:T(8,128)(2,1)S(1)} %bitcast.162), channel_id=1, source_target_pairs={{0,1},{1,2},{2,3},{3,4},{4,5},{5,6},{6,7},{7,8},{8,9},{9,10},{10,1... | collective-permute-start | bytes 98312 | tf_op jit(solution)/shard_map/ppermute | solution.py:24
  11.0 1.5 convolution_add_fusion.6
  12.6 2.7 %convolution_add_fusion.3 = f32[1024,256]{1,0:T(8,128)} fusion(bf16[1024,512]{1,0:T(8,128)(2,1)} %bitcast.155, bf16[512,256]{1,0:T(8,128)(2,1)} %param.17, f32[256]{0:T(256)S(1)} %bitcast.177), kind=kOutput, calls=%fused_computation.41 | convolution fusion | flops 268697600 | bytes 2360320 | tf_op jit(solution)/shard_map/dot_general | solution.py:62
  15.2 2.7 %convolution_add_fusion = f32[4096,256]{1,0:T(8,128)} fusion(bf16[4096,256]{1,0:T(8,128)(2,1)S(1)} %bitcast.134, bf16[256,256]{1,0:T(8,128)(2,1)S(1)} %copy-done.7, f32[256]{0:T(256)S(1)} %bitcast.168), kind=kOutput, calls=%fused_computation.10 | convolution fusion | flops 537919488 | bytes 6423552 | tf_op jit(solution)/shard_map/dot_general | solution.py:62
  18.0 1.2 fusion.43
  19.2 1.2 convolution_add_fusion.8
  20.4 1.2 convolution_add_fusion.7
  22.6 1.9 %collective-permute-start.2 = (bf16[2,1,64,256]{3,2,1,0:T(8,128)(2,1)S(1)}, bf16[2,1,64,256]{3,2,1,0:T(8,128)(2,1)S(1)}, u32[]{:S(2)}, u32[]{:S(2)}) collective-permute-start(bf16[2,1,64,256]{3,2,1,0:T(8,128)(2,1)S(1)} %get-tuple-element.89), channel_id=1, source_target_pairs={{0,1},{1,2},{2,3},{3,4},{4,5},{5,6},{6,7},{7,8},{8,9},{9,10},{10,1... | collective-permute-start | bytes 196616 | tf_op jit(solution)/shard_map/ppermute | solution.py:24
  24.5 2.4 %collective-permute-start.3 = (bf16[2,1,64,256]{3,2,1,0:T(8,128)(2,1)S(1)}, bf16[2,1,64,256]{3,2,1,0:T(8,128)(2,1)S(1)}, u32[]{:S(2)}, u32[]{:S(2)}) collective-permute-start(bf16[2,1,64,256]{3,2,1,0:T(8,128)(2,1)S(1)} %get-tuple-element.90), channel_id=1, source_target_pairs={{1,0},{2,1},{3,2},{4,3},{5,4},{6,5},{7,6},{8,7},{9,8},{10,9},{11,1... | collective-permute-start | bytes 196616 | tf_op jit(solution)/shard_map/ppermute | solution.py:26
  27.4 2.7 %collective-permute-done.3 = bf16[2,1,64,256]{3,2,1,0:T(8,128)(2,1)S(1)} collective-permute-done((bf16[2,1,64,256]{3,2,1,0:T(8,128)(2,1)S(1)}, bf16[2,1,64,256]{3,2,1,0:T(8,128)(2,1)S(1)}, u32[]{:S(2)}, u32[]{:S(2)}) %collective-permute-start.3) | collective-permute-done | bytes 65568 | tf_op jit(solution)/shard_map/ppermute | solution.py:26
  30.4 1.3 fusion.48
  31.7 1.3 convolution_add_fusion.5
  32.9 1.3 convolution_add_fusion.4
  37.6 1.9 %collective-permute-start.4 = (bf16[2,1,128,256]{3,1,2,0:T(2,128)(2,1)S(1)}, bf16[2,1,128,256]{3,1,2,0:T(2,128)(2,1)S(1)}, u32[]{:S(2)}, u32[]{:S(2)}) collective-permute-start(bf16[2,1,128,256]{3,1,2,0:T(2,128)(2,1)S(1)} %get-tuple-element.66), channel_id=1, source_target_pairs={{0,1},{1,2},{2,3},{3,4},{4,5},{5,6},{6,7},{7,8},{8,9},{9,10},{10,1... | collective-permute-start | bytes 393224 | tf_op jit(solution)/shard_map/ppermute | solution.py:24
  39.5 2.4 %collective-permute-start.5 = (bf16[2,1,128,256]{3,1,2,0:T(2,128)(2,1)S(1)}, bf16[2,1,128,256]{3,1,2,0:T(2,128)(2,1)S(1)}, u32[]{:S(2)}, u32[]{:S(2)}) collective-permute-start(bf16[2,1,128,256]{3,1,2,0:T(2,128)(2,1)S(1)} %get-tuple-element.67), channel_id=1, source_target_pairs={{1,0},{2,1},{3,2},{4,3},{5,4},{6,5},{7,6},{8,7},{9,8},{10,9},{11,1... | collective-permute-start | bytes 393224 | tf_op jit(solution)/shard_map/ppermute | solution.py:26
  42.8 4.4 %collective-permute-done.5 = bf16[2,1,128,256]{3,1,2,0:T(2,128)(2,1)S(1)} collective-permute-done((bf16[2,1,128,256]{3,1,2,0:T(2,128)(2,1)S(1)}, bf16[2,1,128,256]{3,1,2,0:T(2,128)(2,1)S(1)}, u32[]{:S(2)}, u32[]{:S(2)}) %collective-permute-start.5) | collective-permute-done | bytes 131104 | tf_op jit(solution)/shard_map/ppermute | solution.py:26
  48.0 1.4 fusion.26
  49.4 1.5 pad_slice_fusion.5
  51.0 2.7 %fusion.21 = (bf16[2,4,128,768]{3,1,2,0:T(4,128)(2,1)S(1)}, bf16[2,4,128,768]{3,1,2,0:T(4,128)(2,1)S(1)}, bf16[2,4,128,768]{3,1,2,0:T(4,128)(2,1)S(1)}) fusion(bf16[2,4,128,256]{3,1,2,0:T(4,128)(2,1)S(1)} %fusion.31, bf16[2,1,128,256]{3,1,2,0:T(2,128)(2,1)S(1)} %collective-permute-done.4, bf16[2,4,128,256]{3,1,2,0:T(4,128)(2,1)S(1)} %get-tuple-element.54, ...), kind=kLoop, calls=%fused_computation.37 | loop fusion | flops 17301504 | bytes 8650752 | tf_op jit(solution)/shard_map/concatenate | solution.py:74
  54.1 1.6 fusion.52
  55.9 1.6 fusion.50
  60.0 2.4 %copy.89 = f32[2,8,128,2,256]{4,1,3,2,0:T(8,128)S(1)} copy(f32[2,8,128,2,256]{4,2,1,0,3:T(8,128)S(1)} %pad_maximum_fusion.3) | data formatting | bytes 8388608 | tf_op jit(solution)/shard_map/stack | solution.py:44
  62.5 2.8 %fusion.11 = bf16[2,8,256,256]{3,1,2,0:T(8,128)(2,1)S(1)} fusion(f32[2,8,256,256]{3,1,2,0:T(8,128)S(1)} %bitcast.140, f32[2,8,256,256]{3,2,1,0:T(8,128)S(1)} %bitcast.137), kind=kLoop, calls=%fused_computation.20 | loop fusion | flops 2097152 | bytes 10485760 | tf_op jit(solution)/shard_map/convert_element_type | solution.py:134
  65.2 1.6 fusion.103
  66.9 1.9 %collective-permute-start.6 = (bf16[2,1,256,256]{3,1,2,0:T(2,128)(2,1)}, bf16[2,1,256,256]{3,1,2,0:T(2,128)(2,1)}, u32[]{:S(2)}, u32[]{:S(2)}) collective-permute-start(bf16[2,1,256,256]{3,1,2,0:T(2,128)(2,1)} %get-tuple-element.45), channel_id=1, source_target_pairs={{0,1},{1,2},{2,3},{3,4},{4,5},{5,6},{6,7},{7,8},{8,9},{9,10},{10,1... | collective-permute-start | bytes 786440 | tf_op jit(solution)/shard_map/ppermute | solution.py:24
  68.8 15.1 %collective-permute-start.7 = (bf16[2,1,256,256]{3,1,2,0:T(2,128)(2,1)}, bf16[2,1,256,256]{3,1,2,0:T(2,128)(2,1)}, u32[]{:S(2)}, u32[]{:S(2)}) collective-permute-start(bf16[2,1,256,256]{3,1,2,0:T(2,128)(2,1)} %get-tuple-element.46), channel_id=1, source_target_pairs={{1,0},{2,1},{3,2},{4,3},{5,4},{6,5},{7,6},{8,7},{9,8},{10,9},{11,1... | collective-permute-start | bytes 786440 | tf_op jit(solution)/shard_map/ppermute | solution.py:26
  83.9 1.6 fusion.22
  85.6 1.3 copy.100
  86.9 3.1 %reshape_reshape.27 = f32[2,512,32,8]{1,0,3,2:T(2,128)} reshape(f32[1024,256]{0,1:T(8,128)} %copy.100) | data formatting | bytes 2097152 | tf_op jit(solution)/shard_map/reshape;reshape | solution.py:90
  90.0 2.0 %fusion.99 = (f32[2,32]{0,1:T(8,128)S(1)}, f32[2,32]{0,1:T(8,128)S(1)}) fusion(f32[2,512,32,8]{1,0,3,2:T(2,128)} %reshape_reshape.27), kind=kLoop, calls=%fused_computation.192 | loop fusion | flops 786304 | bytes 1049088 | tf_op jit(solution)/shard_map/reduce_sum | solution.py:91
  92.7 4.3 %fusion.10 = bf16[2,10,258,256]{3,1,2,0:T(8,128)(2,1)S(1)} fusion(bf16[2,1,256,256]{3,1,2,0:T(2,128)(2,1)} %collective-permute-done.7, bf16[2,8,256,256]{3,1,2,0:T(8,128)(2,1)S(1)} %fusion.11, bf16[2,1,256,256]{3,1,2,0:T(2,128)(2,1)} %collective-permute-done.6), kind=kLoop, calls=%fused_computation.17 | loop fusion | flops 15851520 | bytes 5263360 | tf_op jit(solution)/shard_map/concatenate | solution.py:22
  97.0 4.4 %fusion.102 = (bf16[2,8,256,256]{3,1,2,0:T(8,128)(2,1)S(1)}, bf16[2,8,256,256]{3,1,2,0:T(8,128)(2,1)S(1)}, bf16[2,8,256,256]{3,1,2,0:T(8,128)(2,1)}, bf16[2,8,25...) fusion(bf16[2,10,258,256]{3,1,2,0:T(8,128)(2,1)S(1)} %fusion.10), kind=kLoop, calls=%fused_computation.195 | loop fusion | bytes 25165824 | tf_op jit(solution)/shard_map/slice | solution.py:76
  101.4 9.6 %fusion.4 = (bf16[2,8,256,768]{3,1,2,0:T(8,128)(2,1)S(1)}, bf16[2,8,256,768]{3,1,2,0:T(8,128)(2,1)}, bf16[2,8,256,768]{3,1,2,0:T(8,128)(2,1)}) fusion(bf16[2,8,256,256]{3,1,2,0:T(8,128)(2,1)S(1)} %fusion.11, bf16[2,1,256,256]{3,1,2,0:T(2,128)(2,1)} %collective-permute-done.6, bf16[2,8,256,256]{3,1,2,0:T(8,128)(2,1)} %get-tuple-element.40, ...), kind=kLoop, calls=%fused_computation.8 | loop fusion | flops 69206016 | bytes 34078720 | tf_op jit(solution)/shard_map/concatenate | solution.py:74
  110.9 1.4 copy.91
  112.3 4.2 %copy.92 = bf16[2,8,256,768]{3,2,1,0:T(8,128)(2,1)S(1)} copy(bf16[2,8,256,768]{3,1,2,0:T(8,128)(2,1)} %get-tuple-element.43) | data formatting | bytes 12582912 | tf_op jit(solution)/shard_map/concatenate | solution.py:74
  116.5 2.8 %fusion.57 = f32[4096,256]{1,0:T(8,128)S(1)} fusion(bf16[4096,768]{1,0:T(8,128)(2,1)S(1)} %bitcast.138, bf16[4,3,768,256]{3,2,1,0:T(8,128)(2,1)} %param.21), kind=kOutput, calls=%fused_computation.105 | convolution fusion | flops 1610612736 | bytes 10878976 | tf_op jit(solution)/shard_map/dot_general | solution.py:82
  119.3 4.2 %copy.93 = bf16[2,8,256,768]{3,2,1,0:T(8,128)(2,1)S(1)} copy(bf16[2,8,256,768]{3,1,2,0:T(8,128)(2,1)} %get-tuple-element.44) | data formatting | bytes 12582912 | tf_op jit(solution)/shard_map/concatenate | solution.py:74
  123.5 2.8 %fusion.55 = f32[4096,256]{1,0:T(8,128)S(1)} fusion(bf16[4096,768]{1,0:T(8,128)(2,1)S(1)} %bitcast.139, bf16[4,3,768,256]{3,2,1,0:T(8,128)(2,1)} %param.21), kind=kOutput, calls=%fused_computation.103 | convolution fusion | flops 1610612736 | bytes 10878976 | tf_op jit(solution)/shard_map/dot_general | solution.py:82
  126.3 5.1 %fusion.5 = f32[4096,256]{1,0:T(8,128)} fusion(f32[4096,256]{1,0:T(8,128)S(1)} %fusion.55, f32[4096,256]{1,0:T(8,128)S(1)} %fusion.57, bf16[4096,768]{1,0:T(8,128)(2,1)S(1)} %bitcast.136, bf16[4,3,768,256]{3,2,1,0:T(8,128)(2,1)} %param.21), kind=kOutput, calls=%fused_computation.12 | convolution fusion | flops 1612709888 | bytes 19267584 | tf_op jit(solution)/shard_map/dot_general | solution.py:82
  131.4 5.6 %copy.94 = f32[4096,256]{0,1:T(8,128)} copy(f32[4096,256]{1,0:T(8,128)} %fusion.5) | data formatting | bytes 8388608 | tf_op jit(solution)/shard_map/add | solution.py:82
  137.1 6.8 %reshape_reshape.25 = f32[2,2048,32,8]{1,0,3,2:T(2,128)} reshape(f32[4096,256]{0,1:T(8,128)} %copy.94) | data formatting | bytes 8388608 | tf_op jit(solution)/shard_map/reshape;reshape | solution.py:90
  143.9 5.2 %fusion.98 = (f32[2,32]{0,1:T(8,128)S(1)}, f32[2,32]{0,1:T(8,128)S(1)}) fusion(f32[2,2048,32,8]{1,0,3,2:T(2,128)} %reshape_reshape.25), kind=kLoop, calls=%fused_computation.191 | loop fusion | flops 3145600 | bytes 4194816 | tf_op jit(solution)/shard_map/reduce_sum | solution.py:91
  149.2 12.3 %all-reduce.5 = (f32[2,32]{1,0:T(2,128)S(1)}, f32[2,32]{1,0:T(2,128)S(1)}, f32[2,32]{1,0:T(2,128)S(1)}, f32[2,32]{1,0:T(2,128)S(1)}, f32[2,32]{1,0:T(2,128)S(1)}...) all-reduce(f32[2,32]{1,0:T(2,128)S(1)} %copy.96, ...), channel_id=1, replica_groups=mesh['batch'=8,'rows_0'=4,'rows_1'=4,'rows_2'=2] {'rows_0'}, use_global_device_ids=true, to_apply=%region_5.6 | all-reduce | flops 512 | bytes 4096 | tf_op jit(solution)/shard_map/psum | solution.py:34
  161.5 8.6 %all-reduce.4 = (f32[2,32]{1,0:T(2,128)S(1)}, f32[2,32]{1,0:T(2,128)S(1)}, f32[2,32]{1,0:T(2,128)S(1)}, f32[2,32]{1,0:T(2,128)S(1)}, f32[2,32]{1,0:T(2,128)S(1)}...) all-reduce(f32[2,32]{1,0:T(2,128)S(1)} %get-tuple-element.20, ...), channel_id=1, replica_groups=mesh['batch'=8,'rows_0'=4,'rows_1'=4,'rows_2'=2] {'rows_1'}, use_global_device_ids=true, to_apply=%region_6.7 | all-reduce | flops 512 | bytes 4096 | tf_op jit(solution)/shard_map/psum | solution.py:34
  170.1 7.4 %all-reduce.6 = (f32[2,32]{1,0:T(2,128)S(1)}, f32[2,32]{1,0:T(2,128)S(1)}, f32[2,32]{1,0:T(2,128)S(1)}, f32[2,32]{1,0:T(2,128)S(1)}, f32[2,32]{1,0:T(2,128)S(1)}...) all-reduce(f32[2,32]{1,0:T(2,128)S(1)} %get-tuple-element.12, ...), channel_id=1, replica_groups=mesh['batch'=8,'rows_0'=4,'rows_1'=4,'rows_2'=2] {'rows_2'}, use_global_device_ids=true, to_apply=%region_7.8 | all-reduce | flops 512 | bytes 4096 | tf_op jit(solution)/shard_map/psum | solution.py:34
  181.2 4.2 %add_convert_fusion = bf16[2,8,256,256]{3,2,1,0:T(8,128)(2,1)} fusion(f32[2,8,256,256]{3,2,1,0:T(8,128)} %bitcast.135, f32[256]{0:T(256)S(1)} %bitcast.172, f32[256]{0:T(256)S(1)} %bitcast.169, f32[2,256]{1,0:T(2,128)S(1)} %mul.222, f32[2,256]{1,0:T(2,128)S(1)} %sub.74), kind=kLoop, calls=%fused_computation.21 | loop fusion | flops 5242880 | bytes 6297600 | tf_op jit(solution)/shard_map/convert_element_type | solution.py:101
  (101 shorter events, 16.1 us)
Async XLA Ops:
  0.6 14.6 %copy-start = (bf16[2,8,256,256]{3,2,1,0:T(8,128)(2,1)S(1)}, bf16[2,8,256,256]{3,2,1,0:T(8,128)(2,1)}, u32[]{:S(2)}) copy-start(bf16[2,8,256,256]{3,2,1,0:T(8,128)(2,1)} %param.12) | copy-start | bytes 6291460
  0.6 14.6 %copy-start.7 = (bf16[256,256]{1,0:T(8,128)(2,1)S(1)}, bf16[256,256]{1,0:T(8,128)(2,1)}, u32[]{:S(2)}) copy-start(bf16[256,256]{1,0:T(8,128)(2,1)} %param.16) | copy-start | bytes 393220
  3.2 14.7 %collective-permute-start.1 = (bf16[2,1,32,256]{3,2,0,1:T(8,128)(2,1)S(1)}, bf16[2,1,32,256]{3,2,0,1:T(8,128)(2,1)S(1)}, u32[]{:S(2)}, u32[]{:S(2)}) collective-permute-start(bf16[2,1,32,256]{3,2,0,1:T(8,128)(2,1)S(1)} %bitcast.161), channel_id=1, source_target_pairs={{1,0},{2,1},{3,2},{4,3},{5,4},{6,5},{7,6},{8,7},{9,8},{10,9},{11,1... | collective-permute-start | bytes 98312 | tf_op jit(solution)/shard_map/ppermute | solution.py:26
  8.3 9.6 %collective-permute-start = (bf16[2,1,32,256]{3,2,0,1:T(8,128)(2,1)S(1)}, bf16[2,1,32,256]{3,2,0,1:T(8,128)(2,1)S(1)}, u32[]{:S(2)}, u32[]{:S(2)}) collective-permute-start(bf16[2,1,32,256]{3,2,0,1:T(8,128)(2,1)S(1)} %bitcast.162), channel_id=1, source_target_pairs={{0,1},{1,2},{2,3},{3,4},{4,5},{5,6},{6,7},{7,8},{8,9},{9,10},{10,1... | collective-permute-start | bytes 98312 | tf_op jit(solution)/shard_map/ppermute | solution.py:24
  15.2 2.7 %copy-start.8 = (f32[4,256]{1,0:T(4,128)S(1)}, f32[4,256]{1,0:T(4,128)}, u32[]{:S(2)}) copy-start(f32[4,256]{1,0:T(4,128)} %param.23) | copy-start | bytes 12292
  22.6 4.8 %collective-permute-start.2 = (bf16[2,1,64,256]{3,2,1,0:T(8,128)(2,1)S(1)}, bf16[2,1,64,256]{3,2,1,0:T(8,128)(2,1)S(1)}, u32[]{:S(2)}, u32[]{:S(2)}) collective-permute-start(bf16[2,1,64,256]{3,2,1,0:T(8,128)(2,1)S(1)} %get-tuple-element.89), channel_id=1, source_target_pairs={{0,1},{1,2},{2,3},{3,4},{4,5},{5,6},{6,7},{7,8},{8,9},{9,10},{10,1... | collective-permute-start | bytes 196616 | tf_op jit(solution)/shard_map/ppermute | solution.py:24
  24.5 5.6 %collective-permute-start.3 = (bf16[2,1,64,256]{3,2,1,0:T(8,128)(2,1)S(1)}, bf16[2,1,64,256]{3,2,1,0:T(8,128)(2,1)S(1)}, u32[]{:S(2)}, u32[]{:S(2)}) collective-permute-start(bf16[2,1,64,256]{3,2,1,0:T(8,128)(2,1)S(1)} %get-tuple-element.90), channel_id=1, source_target_pairs={{1,0},{2,1},{3,2},{4,3},{5,4},{6,5},{7,6},{8,7},{9,8},{10,9},{11,1... | collective-permute-start | bytes 196616 | tf_op jit(solution)/shard_map/ppermute | solution.py:26
  35.2 1.2 copy-start.5
  35.5 6.5 %copy-start.6 = (f32[2,128,32,8]{1,0,3,2:T(2,128)S(1)}, f32[2,128,32,8]{1,0,3,2:T(2,128)}, u32[]{:S(2)}) copy-start(f32[2,128,32,8]{1,0,3,2:T(2,128)} %reshape_reshape.29) | copy-start | bytes 786436
  37.6 5.2 %collective-permute-start.4 = (bf16[2,1,128,256]{3,1,2,0:T(2,128)(2,1)S(1)}, bf16[2,1,128,256]{3,1,2,0:T(2,128)(2,1)S(1)}, u32[]{:S(2)}, u32[]{:S(2)}) collective-permute-start(bf16[2,1,128,256]{3,1,2,0:T(2,128)(2,1)S(1)} %get-tuple-element.66), channel_id=1, source_target_pairs={{0,1},{1,2},{2,3},{3,4},{4,5},{5,6},{6,7},{7,8},{8,9},{9,10},{10,1... | collective-permute-start | bytes 393224 | tf_op jit(solution)/shard_map/ppermute | solution.py:24
  39.5 7.7 %collective-permute-start.5 = (bf16[2,1,128,256]{3,1,2,0:T(2,128)(2,1)S(1)}, bf16[2,1,128,256]{3,1,2,0:T(2,128)(2,1)S(1)}, u32[]{:S(2)}, u32[]{:S(2)}) collective-permute-start(bf16[2,1,128,256]{3,1,2,0:T(2,128)(2,1)S(1)} %get-tuple-element.67), channel_id=1, source_target_pairs={{1,0},{2,1},{3,2},{4,3},{5,4},{6,5},{7,6},{8,7},{9,8},{10,9},{11,1... | collective-permute-start | bytes 393224 | tf_op jit(solution)/shard_map/ppermute | solution.py:26
  60.0 2.4 %copy-start.2 = (f32[4096,256]{1,0:T(8,128)S(1)}, f32[4096,256]{1,0:T(8,128)}, u32[]{:S(2)}) copy-start(f32[4096,256]{1,0:T(8,128)} %convolution_add_fusion) | copy-start | bytes 12582916
  66.9 25.8 %collective-permute-start.6 = (bf16[2,1,256,256]{3,1,2,0:T(2,128)(2,1)}, bf16[2,1,256,256]{3,1,2,0:T(2,128)(2,1)}, u32[]{:S(2)}, u32[]{:S(2)}) collective-permute-start(bf16[2,1,256,256]{3,1,2,0:T(2,128)(2,1)} %get-tuple-element.45), channel_id=1, source_target_pairs={{0,1},{1,2},{2,3},{3,4},{4,5},{5,6},{6,7},{7,8},{8,9},{9,10},{10,1... | collective-permute-start | bytes 786440 | tf_op jit(solution)/shard_map/ppermute | solution.py:24
  68.8 23.9 %collective-permute-start.7 = (bf16[2,1,256,256]{3,1,2,0:T(2,128)(2,1)}, bf16[2,1,256,256]{3,1,2,0:T(2,128)(2,1)}, u32[]{:S(2)}, u32[]{:S(2)}) collective-permute-start(bf16[2,1,256,256]{3,1,2,0:T(2,128)(2,1)} %get-tuple-element.46), channel_id=1, source_target_pairs={{1,0},{2,1},{3,2},{4,3},{5,4},{6,5},{7,6},{8,7},{9,8},{10,9},{11,1... | collective-permute-start | bytes 786440 | tf_op jit(solution)/shard_map/ppermute | solution.py:26
  85.5 11.5 %copy-start.3 = (f32[1024,256]{1,0:T(8,128)}, f32[1024,256]{1,0:T(8,128)S(1)}, u32[]{:S(2)}) copy-start(f32[1024,256]{1,0:T(8,128)S(1)} %fusion.22) | copy-start | bytes 3145732
  143.8 5.4 %copy-start.9 = (f32[2,32]{1,0:T(2,128)S(1)}, f32[2,32]{1,0:T(2,128)}, u32[]{:S(2)}) copy-start(f32[2,32]{1,0:T(2,128)} %copy.101) | copy-start | bytes 772
  143.8 36.4 %copy-start.4 = (f32[1024,256]{1,0:T(8,128)S(1)}, f32[1024,256]{1,0:T(8,128)}, u32[]{:S(2)}) copy-start(f32[1024,256]{1,0:T(8,128)} %copy-done.3) | copy-start | bytes 3145732
  178.9 6.5 %copy-start.1 = (bf16[2,8,256,256]{3,2,1,0:T(8,128)(2,1)S(1)}, bf16[2,8,256,256]{3,2,1,0:T(8,128)(2,1)}, u32[]{:S(2)}) copy-start(bf16[2,8,256,256]{3,2,1,0:T(8,128)(2,1)} %param.12) | copy-start | bytes 6291460
where the time goes:
time: 188 us; the launch traced here: 186 us
  local copies, waits for them, and re-layouts  44.8 us (24%)
  other arithmetic  39.5 us (21%)
  starting transfers between devices  32.7 us (17%)
  matrix products  31.3 us (17%)
  blocking collectives  28.3 us (15%)
  waiting for transfers between devices  7.57 us (4%)
    psum x3, blocking collectives, one_axis_at_a_time(): return functools.reduce(lax.psum, axes, shard)  28.3 us
    ppermute x4, starting transfers between devices, with_halo(): lax.ppermute(head, axis, [((i + 1) % count, i) for i in range(ends)])  25 us
    dot_general x12, matrix products, conv_three(): jnp.dot(stacked.reshape(-1, 3 * channels), weight[tap_row], preferred_ele...  22.8 us
    concatenate x4, other arithmetic, conv_three(): jnp.concatenate([band_rows[:, :, 0:width_cells], band_rows[:, :, 1:width_...  12.4 us
    another operation x4, local copies, waits for them, and re-layouts, group_sums(): grouped = conv_out.reshape(dims_all[0], -1, GROUPS, dims_all[3] // GROUPS)  10.9 us
    concatenate x6, local copies, waits for them, and re-layouts, conv_three(): jnp.concatenate([band_rows[:, :, 0:width_cells], band_rows[:, :, 1:width_...  10.3 us
    dot_general x4, matrix products, lateral(): jnp.dot(flattened, weight, preferred_element_type=jnp.float32) + bias_row  8.43 us
    reduce_sum x4, other arithmetic, group_sums(): jnp.sum(grouped, axis=(1, 3))  7.79 us
  transfers between devices with their start and end apart: 8, of which 3 were waited for; matrix products, arithmetic and copies ran while one was open for 9% of the time, Pallas kernels for 0%

commit v1 on v0

v1 whole, which is shorter than its diff:
```python
import jax
import jax.numpy as jnp
from jax import lax
from jax.experimental import pallas as pl
from jax.experimental.pallas import tpu as pltpu
from jax.sharding import PartitionSpec as P

MESH = pl.DeviceIdType.MESH
F32 = jnp.float32
BF16 = jnp.bfloat16
EPSILON = 1e-05
CHANNELS = 256
GROUP = 8
IMAGES = 2
COLS = (256, 128, 64, 32)
STRIP = (8, 4, 2, 1)
DEPTH = (256, 512, 1024, 2048)


def interpolation(cols, coarse_rows, pieces, width):
    coarse = cols // 2
    lanes = lax.broadcasted_iota(jnp.int32, (cols, width), 1)
    fine = lax.broadcasted_iota(jnp.int32, (cols, width), 0)
    block = lax.div(lanes, coarse)
    column = lax.rem(lanes, coarse)
    near = lax.div(fine, 2)
    far = jnp.clip(near + 2 * lax.rem(fine, 2) - 1, 0, coarse - 1)
    taps = jnp.where(column == near, 0.75, 0.0) + jnp.where(column == far, 0.25, 0.0)
    result = []
    for pairs in pieces:
        weight = jnp.zeros((cols, width), F32)
        for row, value in pairs:
            weight = jnp.where(block == row, value, weight)
        result.append((taps * weight).astype(BF16))
    return result


def lane_groups(values):
    lane = lax.broadcasted_iota(jnp.int32, values.shape, 1)
    for step in (1, 2, 4):
        upper = lax.rem(lax.div(lane, step), 2) == 1
        values = values + jnp.where(
            upper, pltpu.roll(values, step, axis=1), pltpu.roll(values, 128 - step, axis=1)
        )
    return values


def encode(stats, slot):
    rows = [
        jnp.sum(stats[image, kind], axis=0, keepdims=True)
        for image in range(IMAGES)
        for kind in range(2)
    ]
    packed = jnp.concatenate([r[:, :128] for r in rows] + [r[:, 128:] for r in rows], 0)
    packed = lane_groups(packed)
    lane = lax.broadcasted_iota(jnp.int32, packed.shape, 1)
    which = lax.broadcasted_iota(jnp.int32, packed.shape, 0)
    packed = jnp.where(lax.rem(lane, 8) == lax.rem(which, 4) + slot, packed, 0.0)
    return jnp.concatenate(
        [
            jnp.sum(packed[0:4], axis=0, keepdims=True),
            jnp.sum(packed[4:8], axis=0, keepdims=True),
        ],
        0,
    )


def decode(totals, slot):
    spread = jnp.concatenate([totals[0:1]] * 4 + [totals[1:2]] * 4, 0)
    lane = lax.broadcasted_iota(jnp.int32, spread.shape, 1)
    which = lax.broadcasted_iota(jnp.int32, spread.shape, 0)
    spread = jnp.where(lax.rem(lane, 8) == lax.rem(which, 4) + slot, spread, 0.0)
    spread = lane_groups(spread)
    row = lambda q: jnp.concatenate([spread[q : q + 1], spread[q + 4 : q + 5]], 1)
    return [(row(2 * image), row(2 * image + 1)) for image in range(IMAGES)]


def kernel(strips, *refs):
    (f2, f3, f4, f5, w2, w3, w4, w5, bias, smooth, gain, shift) = refs[:12]
    outs = refs[12:16]
    (
        f2v, f3v, f4v, f5v, w2v, w3v, w4v, w5v, biasv, smv, gainv, shiftv,
        xc2, xc3, xc4, xc5,
        t2, t3, t4,
        lat3, lat4,
        e5, e4, e3,
        r5, r4, r3, r2,
        rb2, rb3, rb4, rb5,
        cv2, cv3, cv4, cv5,
        stats,
        sendA, sendB, recvA, recvB,
        in_sem, edge_send, edge_recv, all_send, all_recv,
    ) = refs[16:]
    batch = lax.axis_index("batch")
    me = lax.axis_index("rows")
    peers = strips - 1
    above = lax.rem(me + strips - 1, strips)
    below = lax.rem(me + 1, strips)

    pairs = (
        (f5, f5v), (w5, w5v), (bias, biasv), (f4, f4v), (w4, w4v), (f3, f3v), (w3, w3v),
        (f2, f2v), (w2, w2v), (smooth.at[0], smv.at[0]), (smooth.at[1], smv.at[1]),
        (smooth.at[2], smv.at[2]), (smooth.at[3], smv.at[3]), (gain, gainv), (shift, shiftv),
    )
    loads = [pltpu.make_async_copy(s, d, in_sem.at[i]) for i, (s, d) in enumerate(pairs)]
    for load in loads:
        load.start()
    (lf5, lw5, lb, lf4, lw4, lf3, lw3, lf2, lw2, ls2, ls3, ls4, ls5, lg, lsh) = loads

    barrier = pltpu.get_barrier_semaphore()

    @pl.loop(1, strips)
    def _(k):
        pl.semaphore_signal(
            barrier, inc=1, device_id=(batch, lax.rem(me + k, strips)), device_id_type=MESH
        )

    first = me == 0
    last = me == strips - 1
    keep_top = jnp.where(first, 0.0, 1.0)
    keep_bottom = jnp.where(last, 0.0, 1.0)
    top_far = jnp.where(first, 0.0, 0.25)
    top_near = jnp.where(first, 1.0, 0.75)
    bottom_far = jnp.where(last, 0.0, 0.25)
    bottom_near = jnp.where(last, 1.0, 0.75)

    blocks = interpolation(
        64, 3,
        (
            ((0, 0.75), (1, 0.25)),
            ((0, top_far), (1, top_near)),
            ((1, bottom_near), (2, bottom_far)),
            ((1, 0.25), (2, 0.75)),
        ),
        128,
    )
    for i, block in enumerate(blocks):
        t4[64 * i : 64 * i + 64, :] = block
    blocks = interpolation(
        128, 4,
        (
            ((0, top_far), (1, top_near)),
            ((1, 0.75), (2, 0.25)),
            ((1, 0.25), (2, 0.75)),
            ((2, bottom_near), (3, bottom_far)),
            ((0, 0.75), (1, 0.25)),
            ((2, 0.25), (3, 0.75)),
        ),
        256,
    )
    for i, block in enumerate(blocks):
        t3[128 * i : 128 * i + 128, :] = block
    blocks = interpolation(
        256, 2,
        (
            ((0, 0.75), (1, 0.25)),
            ((0, 0.25), (1, 0.75)),
            ((0, top_far), (1, top_near)),
            ((0, bottom_near), (1, bottom_far)),
        ),
        256,
    )
    for place, which in ((0, 0), (1, 1), (2, 0), (3, 2), (4, 3), (5, 1)):
        t2[256 * place : 256 * place + 256, :] = blocks[which]

    for rb, cols in ((rb2, 256), (rb3, 128), (rb4, 64), (rb5, 32)):
        for copy in range(rb.shape[0]):
            for half in range(2):
                rb[copy, half, 0:8, :] = jnp.zeros((8, 128), F32)
                rb[copy, half, cols + 8 : cols + 16, :] = jnp.zeros((8, 128), F32)
    stats[...] = jnp.zeros_like(stats)

    def put_row(rb, copy, target, values):
        cols = values.shape[0]
        for half in range(2):
            rb[copy, half, 8 : 8 + cols, :] = values[:, 128 * half : 128 * half + 128]
        for tap in range(3):
            for half in range(2):
                target[:, 256 * tap + 128 * half : 256 * tap + 128 * half + 128] = rb[
                    copy, half, 7 + tap : 7 + tap + cols, :
                ].astype(BF16)

    def dot(a, b):
        return jnp.dot(a, b, preferred_element_type=F32)

    def edge(level, side, source, target, peer):
        return pltpu.make_async_remote_copy(
            src_ref=source,
            dst_ref=target,
            send_sem=edge_send.at[level, side],
            recv_sem=edge_recv.at[level, side],
            device_id=(batch, peer),
            device_id_type=MESH,
        )

    edges5 = (edge(3, 0, e5, r5.at[1], above), edge(3, 1, e5, r5.at[0], below))
    edges4 = (edge(2, 0, e4.at[0], r4.at[1], above), edge(2, 1, e4.at[1], r4.at[0], below))
    edges3 = (edge(1, 0, e3.at[0], r3.at[1], above), edge(1, 1, e3.at[1], r3.at[0], below))
    edges2 = (
        edge(0, 0, f2v.at[:, 0], r2.at[1], above),
        edge(0, 1, f2v.at[:, 7], r2.at[0], below),
    )

    lf5.wait()
    lw5.wait()
    lb.wait()
    merged = dot(f5v[...].reshape(64, 2048), w5v[...]) + biasv[3:4, :]
    e5[...] = merged.reshape(2, 32, 256).astype(BF16)
    pl.semaphore_wait(barrier, peers)
    for image in range(IMAGES):
        put_row(rb5, image, xc5.at[image, 1], merged[32 * image : 32 * image + 32])
    for copy in edges5:
        copy.start()

    lf4.wait()
    lw4.wait()
    flat = dot(f4v[...].reshape(256, 1024), w4v[...]) + biasv[2:3, :]
    for image in range(IMAGES):
        for row in range(2):
            part = flat[(2 * image + row) * 64 : (2 * image + row) * 64 + 64]
            e4[row, image] = part.astype(BF16)
            lat4[image, row] = part
    for copy in edges4:
        copy.start()

    lf3.wait()
    lw3.wait()
    for image in range(IMAGES):
        flat = dot(f3v[image].reshape(512, 512), w3v[...]) + biasv[1:2, :]
        e3[0, image] = flat[0:128].astype(BF16)
        e3[1, image] = flat[384:512].astype(BF16)
        lat3[image] = flat
    for copy in edges3:
        copy.start()
    lf2.wait()
    for copy in edges2:
        copy.start()

    for copy in edges5:
        copy.wait_recv()
    for image in range(IMAGES):
        put_row(rb5, image, xc5.at[image, 0], r5[0, image].astype(F32) * keep_top)
        put_row(rb5, 2 + image, xc5.at[image, 2], r5[1, image].astype(F32) * keep_bottom)
    for copy in edges4:
        copy.wait_recv()
    for image in range(IMAGES):
        coarse = jnp.concatenate(
            [xc5[image, :, :, 256:512].reshape(96, 256), jnp.zeros((32, 256), BF16)], 0
        )
        up = dot(t4[...], coarse)
        put_row(rb4, 0, xc4.at[image, 0], (up[0:64] + r4[0, image].astype(F32)) * keep_top)
        put_row(rb4, 1, xc4.at[image, 1], up[64:128] + lat4[image, 0])
        put_row(rb4, 2, xc4.at[image, 2], up[128:192] + lat4[image, 1])
        put_row(rb4, 3, xc4.at[image, 3], (up[192:256] + r4[1, image].astype(F32)) * keep_bottom)

    for image in range(IMAGES):
        up = dot(t3[0:512, :], xc4[image, :, :, 256:512].reshape(256, 256)) + lat3[image]
        for row in range(4):
            put_row(rb3, row, xc3.at[image, 1 + row], up[128 * row : 128 * row + 128])

    lw2.wait()

    def pair(image, p, features, weights):
        left = jnp.concatenate([features, weights], 1)
        coarse = xc3[image, pl.ds(p + 1, 2), :, 256:512].reshape(256, 256)
        right = jnp.concatenate([w2v[...], coarse], 0)
        return dot(left, right) + biasv[0:1, :]

    @pl.loop(0, IMAGES)
    def _(image):
        for p in range(3):
            both = pair(
                image, p, f2v[image, 2 * p + 1 : 2 * p + 3].reshape(512, 256), t2[0:512, :]
            )
            put_row(rb2, 0, xc2.at[image, 2 * p + 2], both[0:256])
            put_row(rb2, 1, xc2.at[image, 2 * p + 3], both[256:512])

    def tally(level, image, values):
        tiles = values.reshape(values.shape[0] // 8, 8, 256)
        stats[level, image, 0] += jnp.sum(tiles, axis=0)
        stats[level, image, 1] += jnp.sum(tiles * tiles, axis=0)

    def conv(xc, level, image, row, rows):
        cols = COLS[level]
        total = None
        for tap in range(3):
            band = xc[image, pl.ds(row + tap, rows)].reshape(rows * cols, 768)
            term = dot(band, smv[level, tap])
            total = term if total is None else total + term
        return total

    ls2.wait()

    def conv_two(image, row):
        values = conv(xc2, 0, image, row, 2)
        cv2[image, pl.ds(row * 256, 512), :] = values
        tally(0, image, values)

    @pl.loop(0, IMAGES)
    def _(image):
        @pl.loop(1, 3)
        def _(j):
            conv_two(image, 2 * j)

    for copy in edges3:
        copy.wait_recv()
    for image in range(IMAGES):
        up = dot(t3[512:768, :], xc4[image, :, :, 256:512].reshape(256, 256))
        put_row(rb3, 0, xc3.at[image, 0], (up[0:128] + r3[0, image].astype(F32)) * keep_top)
        put_row(rb3, 1, xc3.at[image, 5], (up[128:256] + r3[1, image].astype(F32)) * keep_bottom)
    for copy in edges2:
        copy.wait_recv()

    @pl.loop(0, IMAGES)
    def _(image):
        both = pair(
            image, -1,
            jnp.concatenate([r2[0, image], f2v[image, 0]], 0), t2[512:1024, :],
        )
        put_row(rb2, 0, xc2.at[image, 0], both[0:256] * keep_top)
        put_row(rb2, 1, xc2.at[image, 1], both[256:512])
        both = pair(
            image, 3,
            jnp.concatenate([f2v[image, 7], r2[1, image]], 0), t2[1024:1536, :],
        )
        put_row(rb2, 2, xc2.at[image, 8], both[0:256])
        put_row(rb2, 3, xc2.at[image, 9], both[256:512] * keep_bottom)

    @pl.loop(0, IMAGES)
    def _(image):
        @pl.loop(0, 2)
        def _(j):
            conv_two(image, 6 * j)

    def everyone(source, target, which):
        def copy_to(k):
            return pltpu.make_async_remote_copy(
                src_ref=source,
                dst_ref=target.at[k],
                send_sem=all_send.at[which, k],
                recv_sem=all_recv.at[which, k],
                device_id=(batch, lax.rem(me + 1 + k, strips)),
                device_id_type=MESH,
            )

        return copy_to

    sendA[...] = encode(stats.at[0], 0)
    copyA = everyone(sendA, recvA, 0)
    pl.loop(0, peers)(lambda k: copyA(k).start())

    ls3.wait()
    ls4.wait()
    ls5.wait()
    values = None
    for tap in range(3):
        term = dot(xc5[:, tap].reshape(64, 768), smv[3, tap])
        values = term if values is None else values + term
    cv5[...] = values
    for image in range(IMAGES):
        tally(3, image, values[32 * image : 32 * image + 32])
    values = None
    for tap in range(3):
        term = dot(xc4[:, tap : tap + 2].reshape(256, 768), smv[2, tap])
        values = term if values is None else values + term
    cv4[...] = values
    for image in range(IMAGES):
        tally(2, image, values[128 * image : 128 * image + 128])

    @pl.loop(0, IMAGES)
    def _(image):
        values = conv(xc3, 1, image, 0, 4)
        cv3[image] = values
        tally(1, image, values)

    sendB[...] = jnp.concatenate([encode(stats.at[1], 0) + encode(stats.at[2], 4),
                                  encode(stats.at[3], 0)], 0)
    copyB = everyone(sendB, recvB, 1)
    pl.loop(0, peers)(lambda k: copyB(k).start())

    def affine(level, sums, squares):
        entries = float(COLS[level] * strips * STRIP[level] * GROUP)
        mean = sums / entries
        variance = squares / entries - mean * mean
        scale = lax.rsqrt(variance + EPSILON) * gainv[level : level + 1, :]
        return mean, scale, shiftv[level : level + 1, :]

    def normalized(values, terms):
        mean, scale, offset = terms
        return ((values - mean) * scale + offset).astype(BF16)

    lg.wait()
    lsh.wait()
    pl.loop(0, peers)(lambda k: copyA(k).wait_recv())
    totals = sendA[...] + jnp.sum(recvA[...], axis=0)
    for image, (sums, squares) in enumerate(decode(totals, 0)):
        terms = affine(0, sums, squares)

        @pl.loop(0, 8)
        def _(row):
            outs[0][image, row] = normalized(cv2[image, pl.ds(row * 256, 256), :], terms)

    pl.loop(0, peers)(lambda k: copyB(k).wait_recv())
    totals = sendB[...] + jnp.sum(recvB[...], axis=0)
    for level, half, slot in ((1, 0, 0), (2, 0, 4), (3, 2, 0)):
        for image, (sums, squares) in enumerate(decode(totals[half : half + 2], slot)):
            terms = affine(level, sums, squares)
            if level == 1:
                values = cv3[image]
            elif level == 2:
                values = cv4[128 * image : 128 * image + 128]
            else:
                values = cv5[32 * image : 32 * image + 32]
            outs[level][image] = normalized(values, terms).reshape(
                STRIP[level], COLS[level], 256
            )

    for copies in (edges5, edges4, edges3, edges2):
        for copy in copies:
            copy.wait_send()
    pl.loop(0, peers)(lambda k: copyA(k).wait_send())
    pl.loop(0, peers)(lambda k: copyB(k).wait_send())


def solution(mesh):
    strips = mesh.shape["rows"]

    def per_device(*args):
        vmem = pltpu.VMEM
        scratch = [
            vmem((2, 8, 256, 256), BF16), vmem((2, 4, 128, 512), BF16),
            vmem((2, 2, 64, 1024), BF16), vmem((2, 1, 32, 2048), BF16),
            vmem((256, 256), BF16), vmem((512, 256), BF16),
            vmem((1024, 256), BF16), vmem((2048, 256), BF16),
            vmem((4, 256), F32), vmem((4, 3, 768, 256), BF16),
            vmem((4, 256), F32), vmem((4, 256), F32),
            vmem((2, 10, 256, 768), BF16), vmem((2, 6, 128, 768), BF16),
            vmem((2, 4, 64, 768), BF16), vmem((2, 3, 32, 768), BF16),
            vmem((1536, 256), BF16), vmem((768, 256), BF16), vmem((256, 128), BF16),
            vmem((2, 512, 256), F32), vmem((2, 2, 64, 256), F32),
            vmem((2, 32, 256), BF16), vmem((2, 2, 64, 256), BF16), vmem((2, 2, 128, 256), BF16),
            vmem((2, 2, 32, 256), BF16), vmem((2, 2, 64, 256), BF16),
            vmem((2, 2, 128, 256), BF16), vmem((2, 2, 256, 256), BF16),
            vmem((4, 2, 272, 128), F32), vmem((4, 2, 144, 128), F32),
            vmem((4, 2, 80, 128), F32), vmem((4, 2, 48, 128), F32),
            vmem((2, 2048, 256), F32), vmem((2, 512, 256), F32),
            vmem((256, 256), F32), vmem((64, 256), F32),
            vmem((4, 2, 2, 8, 256), F32),
            vmem((2, 128), F32), vmem((4, 128), F32),
            vmem((strips - 1, 2, 128), F32), vmem((strips - 1, 4, 128), F32),
            pltpu.SemaphoreType.DMA((15,)),
            pltpu.SemaphoreType.DMA((4, 2)), pltpu.SemaphoreType.DMA((4, 2)),
            pltpu.SemaphoreType.DMA((2, strips - 1)), pltpu.SemaphoreType.DMA((2, strips - 1)),
        ]
        results = pl.pallas_call(
            lambda *refs: kernel(strips, *refs),
            name="pyramid",
            out_shape=[
                pltpu.VMEM((IMAGES, STRIP[k], COLS[k], CHANNELS), BF16) for k in range(4)
            ],
            in_specs=[pl.BlockSpec(memory_space=pltpu.HBM)] * 12,
            out_specs=[pl.BlockSpec(memory_space=pltpu.VMEM)] * 4,
            scratch_shapes=scratch,
            compiler_params=pltpu.CompilerParams(
                collective_id=0, has_side_effects=True, vmem_limit_bytes=48 << 20
            ),
            cost_estimate=pl.CostEstimate(
                flops=7_430_000_000, bytes_accessed=13_300_000, transcendentals=0
            ),
        )(*(pltpu.with_memory_space_constraint(a, pltpu.HBM) for a in args))
        return tuple(results)

    rows = P("batch", "rows", None, None)
    return jax.shard_map(
        per_device,
        mesh=mesh,
        in_specs=(rows,) * 4 + (P(),) * 8,
        out_specs=(rows,) * 4,
        check_vma=False,
    )
```

time: 188 us -> 35.9 us (0.19); the launches traced: 186 us -> 35.8 us
  local copies, waits for them, and re-layouts: 44.8 us -> 3.38 us
  other arithmetic: 39.5 us -> 0 us
  starting transfers between devices: 32.7 us -> 0 us
  Pallas kernels: 0 us -> 31.8 us
  matrix products: 31.3 us -> 0 us
  blocking collectives: 28.3 us -> 0 us
  waiting for transfers between devices: 7.57 us -> 0 us
    ppermute x8 -> x0, starting transfers between devices: 32.7 us -> none  [the longest x4 25 us: with_halo(): lax.ppermute(head, axis, [((i + 1) % count, i) for i in range(ends)])]
    pallas_call x0 -> x1, Pallas kernels: none -> 31.8 us  [per_device(): pl.pallas_call(lambda *refs: kernel(strips, *refs), name='pyramid', out_s...]
    dot_general x16 -> x0, matrix products: 31.3 us -> none  [the longest x12 22.8 us: conv_three(): jnp.dot(stacked.reshape(-1, 3 * channels), weight[tap_row], preferred_ele...]
    psum x3 -> x0, blocking collectives: 28.3 us -> none  [one_axis_at_a_time(): return functools.reduce(lax.psum, axes, shard)]
    concatenate x8 -> x0, other arithmetic: 18.2 us -> none  [the longest x4 12.4 us: conv_three(): jnp.concatenate([band_rows[:, :, 0:width_cells], band_rows[:, :, 1:width_...]
    another operation x8 -> x0, local copies, waits for them, and re-layouts: 14.6 us -> none  [the longest x4 10.9 us: group_sums(): grouped = conv_out.reshape(dims_all[0], -1, GROUPS, dims_all[3] // GROUPS)]
    concatenate x6 -> x0, local copies, waits for them, and re-layouts: 10.3 us -> none  [conv_three(): jnp.concatenate([band_rows[:, :, 0:width_cells], band_rows[:, :, 1:width_...]
    convert_element_type x7 -> x0, other arithmetic: 10.1 us -> none  [the longest x4 6.51 us: normalize(): (centred.reshape(dims_all) * gain_row + shift_row).astype(jnp.bfloat16)]
  transfers between devices with their start and end apart: 8 -> 0, of which waited for: 3 -> 0; matrix products, arithmetic and copies ran while one was open for 9% -> 0% of each run, Pallas kernels for 0% -> 0%
where the time goes in v1:
time: 35.9 us; the launch traced here: 35.8 us
  Pallas kernels  31.8 us (89%)
  local copies, waits for them, and re-layouts  3.38 us (9%)
  between operations  0.65 us (2%)
    pallas_call x1, Pallas kernels, per_device(): pl.pallas_call(lambda *refs: kernel(strips, *refs), name='pyramid', out_s...  31.8 us
    unnamed x4, local copies, waits for them, and re-layouts  3.38 us

profile of v1, /device:TPU:1, one launch (start us, length us, event | category | flops | bytes accessed | tf_op | source)
XLA Modules:
  0.0 35.8 jit_solution(5125505001760482126)
XLA Ops:
  0.6 31.8 %pyramid.1 = (bf16[2,8,256,256]{3,2,1,0:T(8,128)(2,1)S(1)}, bf16[2,4,128,256]{3,2,1,0:T(8,128)(2,1)S(1)}, bf16[2,2,64,256]{3,2,1,0:T(8,128)(2,1)S(1)}, bf16[2,1,32,256]{3,2,1,0:T(8,128)(2,1)S(1)}) custom-call(bf16[2,8,256,256]{3,2,1,0:T(8,128)(2,1)} %refs_0_.1, bf16[2,4,128,512]{3,2,1,0:T(8,128)(2,1)} %refs_1_.1, bf16[2,2,64,1024]{3,2,1,0:T(8,128)(2,1)} %refs_2_.1, ...), custom_call_target="tpu_custom_call" | custom-call | flops 7430000128 | bytes 13300000 | tf_op jit(solution)/shard_map/pyramid/pallas_call | solution.py:455
  32.4 1.3 %copy.20 = bf16[2,8,256,256]{3,2,1,0:T(8,128)(2,1)} copy(bf16[2,8,256,256]{3,2,1,0:T(8,128)(2,1)S(1)} %get-tuple-element.4) | data formatting | bytes 4194304
  33.7 0.6 %copy.23 = bf16[2,1,32,256]{3,2,1,0:T(8,128)(2,1)} copy(bf16[2,1,32,256]{3,2,1,0:T(8,128)(2,1)S(1)} %get-tuple-element.7) | data formatting | bytes 65536
  34.3 0.7 %copy.22 = bf16[2,2,64,256]{3,2,1,0:T(8,128)(2,1)} copy(bf16[2,2,64,256]{3,2,1,0:T(8,128)(2,1)S(1)} %get-tuple-element.6) | data formatting | bytes 262144
  35.0 0.8 %copy.21 = bf16[2,4,128,256]{3,2,1,0:T(8,128)(2,1)} copy(bf16[2,4,128,256]{3,2,1,0:T(8,128)(2,1)S(1)} %get-tuple-element.5) | data formatting | bytes 1048576

commit v2 on v1

--- a/solution.py
+++ b/solution.py
@@ -45,7 +45,7 @@
     return values
 
 
-def encode(stats, slot):
+def encode(stats):
     rows = [
         jnp.sum(stats[image, kind], axis=0, keepdims=True)
         for image in range(IMAGES)
@@ -55,22 +55,14 @@
     packed = lane_groups(packed)
     lane = lax.broadcasted_iota(jnp.int32, packed.shape, 1)
     which = lax.broadcasted_iota(jnp.int32, packed.shape, 0)
-    packed = jnp.where(lax.rem(lane, 8) == lax.rem(which, 4) + slot, packed, 0.0)
-    return jnp.concatenate(
-        [
-            jnp.sum(packed[0:4], axis=0, keepdims=True),
-            jnp.sum(packed[4:8], axis=0, keepdims=True),
-        ],
-        0,
-    )
-
-
-def decode(totals, slot):
-    spread = jnp.concatenate([totals[0:1]] * 4 + [totals[1:2]] * 4, 0)
+    return jnp.sum(jnp.where(lax.rem(lane, 8) == which, packed, 0.0), axis=0, keepdims=True)
+
+
+def decode(totals):
+    spread = jnp.broadcast_to(totals, (8, 128))
     lane = lax.broadcasted_iota(jnp.int32, spread.shape, 1)
     which = lax.broadcasted_iota(jnp.int32, spread.shape, 0)
-    spread = jnp.where(lax.rem(lane, 8) == lax.rem(which, 4) + slot, spread, 0.0)
-    spread = lane_groups(spread)
+    spread = lane_groups(jnp.where(lax.rem(lane, 8) == which, spread, 0.0))
     row = lambda q: jnp.concatenate([spread[q : q + 1], spread[q + 4 : q + 5]], 1)
     return [(row(2 * image), row(2 * image + 1)) for image in range(IMAGES)]
 
@@ -91,12 +83,28 @@
         sendA, sendB, recvA, recvB,
         in_sem, edge_send, edge_recv, all_send, all_recv,
     ) = refs[16:]
+    current = []
+
+    def phase(name):
+        if current:
+            current.pop().__exit__(None, None, None)
+        if name:
+            current.append(jax.named_scope(name))
+            current[0].__enter__()
+
+    phase("start")
     batch = lax.axis_index("batch")
     me = lax.axis_index("rows")
     peers = strips - 1
     above = lax.rem(me + strips - 1, strips)
     below = lax.rem(me + 1, strips)
 
+    barrier = pltpu.get_barrier_semaphore()
+    for k in [1, strips - 1] + list(range(2, strips - 1)):
+        pl.semaphore_signal(
+            barrier, inc=1, device_id=(batch, lax.rem(me + k, strips)), device_id_type=MESH
+        )
+
     pairs = (
         (f5, f5v), (w5, w5v), (bias, biasv), (f4, f4v), (w4, w4v), (f3, f3v), (w3, w3v),
         (f2, f2v), (w2, w2v), (smooth.at[0], smv.at[0]), (smooth.at[1], smv.at[1]),
@@ -106,14 +114,6 @@
     for load in loads:
         load.start()
     (lf5, lw5, lb, lf4, lw4, lf3, lw3, lf2, lw2, ls2, ls3, ls4, ls5, lg, lsh) = loads
-
-    barrier = pltpu.get_barrier_semaphore()
-
-    @pl.loop(1, strips)
-    def _(k):
-        pl.semaphore_signal(
-            barrier, inc=1, device_id=(batch, lax.rem(me + k, strips)), device_id_type=MESH
-        )
 
     first = me == 0
     last = me == strips - 1
@@ -124,6 +124,7 @@
     bottom_far = jnp.where(last, 0.0, 0.25)
     bottom_near = jnp.where(last, 1.0, 0.75)
 
+    phase("matrices")
     blocks = interpolation(
         64, 3,
         (
@@ -176,9 +177,11 @@
             rb[copy, half, 8 : 8 + cols, :] = values[:, 128 * half : 128 * half + 128]
         for tap in range(3):
             for half in range(2):
-                target[:, 256 * tap + 128 * half : 256 * tap + 128 * half + 128] = rb[
-                    copy, half, 7 + tap : 7 + tap + cols, :
-                ].astype(BF16)
+                target[2 * tap + half] = rb[copy, half, 7 + tap : 7 + tap + cols, :].astype(BF16)
+
+    def middle(xc, image, row, rows):
+        halves = [xc[image, row : row + rows, 2 + half] for half in range(2)]
+        return jnp.concatenate([h.reshape(-1, 128) for h in halves], 1)
 
     def dot(a, b):
         return jnp.dot(a, b, preferred_element_type=F32)
@@ -201,19 +204,25 @@
         edge(0, 1, f2v.at[:, 7], r2.at[0], below),
     )
 
+    phase("wait_load5")
     lf5.wait()
     lw5.wait()
     lb.wait()
+    phase("lat5")
     merged = dot(f5v[...].reshape(64, 2048), w5v[...]) + biasv[3:4, :]
     e5[...] = merged.reshape(2, 32, 256).astype(BF16)
+    phase("barrier")
     pl.semaphore_wait(barrier, peers)
+    phase("put5")
     for image in range(IMAGES):
         put_row(rb5, image, xc5.at[image, 1], merged[32 * image : 32 * image + 32])
     for copy in edges5:
         copy.start()
 
+    phase("wait_load4")
     lf4.wait()
     lw4.wait()
+    phase("lat4")
     flat = dot(f4v[...].reshape(256, 1024), w4v[...]) + biasv[2:3, :]
     for image in range(IMAGES):
         for row in range(2):
@@ -223,8 +232,10 @@
     for copy in edges4:
         copy.start()
 
+    phase("wait_load3")
     lf3.wait()
     lw3.wait()
+    phase("lat3")
     for image in range(IMAGES):
         flat = dot(f3v[image].reshape(512, 512), w3v[...]) + biasv[1:2, :]
         e3[0, image] = flat[0:128].astype(BF16)
@@ -232,20 +243,36 @@
         lat3[image] = flat
     for copy in edges3:
         copy.start()
+    phase("wait_load2")
     lf2.wait()
     for copy in edges2:
         copy.start()
 
+    phase("lat2")
+    lw2.wait()
+
+    @pl.loop(0, IMAGES)
+    def _(image):
+        for part in range(2):
+            cv2[image, 1024 * part : 1024 * part + 1024, :] = (
+                dot(f2v[image, 4 * part : 4 * part + 4].reshape(1024, 256), w2v[...])
+                + biasv[0:1, :]
+            )
+
+    phase("wait_edge5")
     for copy in edges5:
         copy.wait_recv()
+    phase("halo5")
     for image in range(IMAGES):
         put_row(rb5, image, xc5.at[image, 0], r5[0, image].astype(F32) * keep_top)
         put_row(rb5, 2 + image, xc5.at[image, 2], r5[1, image].astype(F32) * keep_bottom)
+    phase("wait_edge4")
     for copy in edges4:
         copy.wait_recv()
+    phase("merge4")
     for image in range(IMAGES):
         coarse = jnp.concatenate(
-            [xc5[image, :, :, 256:512].reshape(96, 256), jnp.zeros((32, 256), BF16)], 0
+            [middle(xc5, image, 0, 3), jnp.zeros((32, 256), BF16)], 0
         )
         up = dot(t4[...], coarse)
         put_row(rb4, 0, xc4.at[image, 0], (up[0:64] + r4[0, image].astype(F32)) * keep_top)
@@ -253,130 +280,145 @@
         put_row(rb4, 2, xc4.at[image, 2], up[128:192] + lat4[image, 1])
         put_row(rb4, 3, xc4.at[image, 3], (up[192:256] + r4[1, image].astype(F32)) * keep_bottom)
 
-    for image in range(IMAGES):
-        up = dot(t3[0:512, :], xc4[image, :, :, 256:512].reshape(256, 256)) + lat3[image]
+    phase("merge3")
+    for image in range(IMAGES):
+        up = dot(t3[0:512, :], middle(xc4, image, 0, 4)) + lat3[image]
         for row in range(4):
             put_row(rb3, row, xc3.at[image, 1 + row], up[128 * row : 128 * row + 128])
 
-    lw2.wait()
-
-    def pair(image, p, features, weights):
-        left = jnp.concatenate([features, weights], 1)
-        coarse = xc3[image, pl.ds(p + 1, 2), :, 256:512].reshape(256, 256)
-        right = jnp.concatenate([w2v[...], coarse], 0)
-        return dot(left, right) + biasv[0:1, :]
-
+    phase("wait_w2")
+
+    def pair(image, p, weights):
+        return dot(weights, middle(xc3, image, p + 1, 2))
+
+    phase("merge2")
     @pl.loop(0, IMAGES)
     def _(image):
         for p in range(3):
-            both = pair(
-                image, p, f2v[image, 2 * p + 1 : 2 * p + 3].reshape(512, 256), t2[0:512, :]
-            )
-            put_row(rb2, 0, xc2.at[image, 2 * p + 2], both[0:256])
-            put_row(rb2, 1, xc2.at[image, 2 * p + 3], both[256:512])
+            both = pair(image, p, t2[0:512, :])
+            for row in range(2):
+                start = 512 * p + 256 + 256 * row
+                put_row(
+                    rb2, row, xc2.at[image, 2 * p + 2 + row],
+                    both[256 * row : 256 * row + 256] + cv2[image, start : start + 256, :],
+                )
 
     def tally(level, image, values):
         tiles = values.reshape(values.shape[0] // 8, 8, 256)
         stats[level, image, 0] += jnp.sum(tiles, axis=0)
         stats[level, image, 1] += jnp.sum(tiles * tiles, axis=0)
 
-    def conv(xc, level, image, row, rows):
-        cols = COLS[level]
+    def product(bands, level):
         total = None
-        for tap in range(3):
-            band = xc[image, pl.ds(row + tap, rows)].reshape(rows * cols, 768)
-            term = dot(band, smv[level, tap])
+        for tap, slabs in enumerate(bands):
+            term = dot(jnp.concatenate(slabs, 1), smv[level, tap])
             total = term if total is None else total + term
         return total
 
+    def conv(xc, level, image, row, rows):
+        return product(
+            [
+                [xc[image, row + tap : row + tap + rows, slab].reshape(-1, 128) for slab in range(6)]
+                for tap in range(3)
+            ],
+            level,
+        )
+
+    phase("wait_s2")
     ls2.wait()
 
     def conv_two(image, row):
         values = conv(xc2, 0, image, row, 2)
-        cv2[image, pl.ds(row * 256, 512), :] = values
+        cv2[image, row * 256 : row * 256 + 512, :] = values
         tally(0, image, values)
 
+    phase("conv2a")
     @pl.loop(0, IMAGES)
     def _(image):
-        @pl.loop(1, 3)
-        def _(j):
-            conv_two(image, 2 * j)
-
+        for row in (2, 4):
+            conv_two(image, row)
+
+    phase("wait_edge3")
     for copy in edges3:
         copy.wait_recv()
-    for image in range(IMAGES):
-        up = dot(t3[512:768, :], xc4[image, :, :, 256:512].reshape(256, 256))
+    phase("halo3")
+    for image in range(IMAGES):
+        up = dot(t3[512:768, :], middle(xc4, image, 0, 4))
         put_row(rb3, 0, xc3.at[image, 0], (up[0:128] + r3[0, image].astype(F32)) * keep_top)
         put_row(rb3, 1, xc3.at[image, 5], (up[128:256] + r3[1, image].astype(F32)) * keep_bottom)
+    phase("wait_edge2")
     for copy in edges2:
         copy.wait_recv()
 
+    phase("merge2b")
     @pl.loop(0, IMAGES)
     def _(image):
-        both = pair(
-            image, -1,
-            jnp.concatenate([r2[0, image], f2v[image, 0]], 0), t2[512:1024, :],
-        )
-        put_row(rb2, 0, xc2.at[image, 0], both[0:256] * keep_top)
-        put_row(rb2, 1, xc2.at[image, 1], both[256:512])
-        both = pair(
-            image, 3,
-            jnp.concatenate([f2v[image, 7], r2[1, image]], 0), t2[1024:1536, :],
-        )
-        put_row(rb2, 2, xc2.at[image, 8], both[0:256])
-        put_row(rb2, 3, xc2.at[image, 9], both[256:512] * keep_bottom)
-
+        both = pair(image, -1, t2[512:1024, :])
+        outside = dot(r2[0, image], w2v[...]) + biasv[0:1, :]
+        put_row(rb2, 0, xc2.at[image, 0], (both[0:256] + outside) * keep_top)
+        put_row(rb2, 1, xc2.at[image, 1], both[256:512] + cv2[image, 0:256, :])
+        both = pair(image, 3, t2[1024:1536, :])
+        outside = dot(r2[1, image], w2v[...]) + biasv[0:1, :]
+        put_row(rb2, 2, xc2.at[image, 8], both[0:256] + cv2[image, 1792:2048, :])
+        put_row(rb2, 3, xc2.at[image, 9], (both[256:512] + outside) * keep_bottom)
+
+    phase("conv2b")
     @pl.loop(0, IMAGES)
     def _(image):
-        @pl.loop(0, 2)
-        def _(j):
-            conv_two(image, 6 * j)
+        for row in (0, 6):
+            conv_two(image, row)
+
+    phase("conv54")
+    ls4.wait()
+    ls5.wait()
+    values = product(
+        [[xc5[:, tap, slab].reshape(64, 128) for slab in range(6)] for tap in range(3)], 3
+    )
+    cv5[...] = values
+    for image in range(IMAGES):
+        tally(3, image, values[32 * image : 32 * image + 32])
+    values = product(
+        [
+            [xc4[:, tap : tap + 2, slab].reshape(256, 128) for slab in range(6)]
+            for tap in range(3)
+        ],
+        2,
+    )
+    cv4[...] = values
+    for image in range(IMAGES):
+        tally(2, image, values[128 * image : 128 * image + 128])
 
     def everyone(source, target, which):
-        def copy_to(k):
-            return pltpu.make_async_remote_copy(
+        return [
+            pltpu.make_async_remote_copy(
                 src_ref=source,
                 dst_ref=target.at[k],
-                send_sem=all_send.at[which, k],
-                recv_sem=all_recv.at[which, k],
+                send_sem=all_send.at[which],
+                recv_sem=all_recv.at[which],
                 device_id=(batch, lax.rem(me + 1 + k, strips)),
                 device_id_type=MESH,
             )
-
-        return copy_to
-
-    sendA[...] = encode(stats.at[0], 0)
-    copyA = everyone(sendA, recvA, 0)
-    pl.loop(0, peers)(lambda k: copyA(k).start())
-
+            for k in range(peers)
+        ]
+
+    phase("encodeA")
+    sendA[...] = jnp.concatenate(
+        [encode(stats.at[0]), encode(stats.at[2]), encode(stats.at[3]), jnp.zeros((1, 128), F32)], 0
+    )
+    for copy in everyone(sendA, recvA, 0):
+        copy.start()
+
+    phase("conv3")
     ls3.wait()
-    ls4.wait()
-    ls5.wait()
-    values = None
-    for tap in range(3):
-        term = dot(xc5[:, tap].reshape(64, 768), smv[3, tap])
-        values = term if values is None else values + term
-    cv5[...] = values
-    for image in range(IMAGES):
-        tally(3, image, values[32 * image : 32 * image + 32])
-    values = None
-    for tap in range(3):
-        term = dot(xc4[:, tap : tap + 2].reshape(256, 768), smv[2, tap])
-        values = term if values is None else values + term
-    cv4[...] = values
-    for image in range(IMAGES):
-        tally(2, image, values[128 * image : 128 * image + 128])
-
-    @pl.loop(0, IMAGES)
-    def _(image):
+    for image in range(IMAGES):
         values = conv(xc3, 1, image, 0, 4)
         cv3[image] = values
         tally(1, image, values)
 
-    sendB[...] = jnp.concatenate([encode(stats.at[1], 0) + encode(stats.at[2], 4),
-                                  encode(stats.at[3], 0)], 0)
-    copyB = everyone(sendB, recvB, 1)
-    pl.loop(0, peers)(lambda k: copyB(k).start())
+    phase("encodeB")
+    sendB[...] = encode(stats.at[1])
+    for copy in everyone(sendB, recvB, 1):
+        copy.start()
 
     def affine(level, sums, squares):
         entries = float(COLS[level] * strips * STRIP[level] * GROUP)
@@ -391,20 +433,16 @@
 
     lg.wait()
     lsh.wait()
-    pl.loop(0, peers)(lambda k: copyA(k).wait_recv())
-    totals = sendA[...] + jnp.sum(recvA[...], axis=0)
-    for image, (sums, squares) in enumerate(decode(totals, 0)):
-        terms = affine(0, sums, squares)
-
-        @pl.loop(0, 8)
-        def _(row):
-            outs[0][image, row] = normalized(cv2[image, pl.ds(row * 256, 256), :], terms)
-
-    pl.loop(0, peers)(lambda k: copyB(k).wait_recv())
-    totals = sendB[...] + jnp.sum(recvB[...], axis=0)
-    for level, half, slot in ((1, 0, 0), (2, 0, 4), (3, 2, 0)):
-        for image, (sums, squares) in enumerate(decode(totals[half : half + 2], slot)):
+    def finish(level, totals):
+        for image, (sums, squares) in enumerate(decode(totals)):
             terms = affine(level, sums, squares)
+            if level == 0:
+
+                @pl.loop(0, 8)
+                def _(row):
+                    outs[0][image, row] = normalized(cv2[image, pl.ds(row * 256, 256), :], terms)
+
+                continue
             if level == 1:
                 values = cv3[image]
             elif level == 2:
@@ -415,11 +453,35 @@
                 STRIP[level], COLS[level], 256
             )
 
+    phase("wait_A")
+    pltpu.make_async_copy(recvA, recvA, all_recv.at[0]).wait()
+    phase("normA")
+    totals = sendA[...] + jnp.sum(recvA[...], axis=0)
+    finish(0, totals[0:1])
+    finish(2, totals[1:2])
+    finish(3, totals[2:3])
+
+    phase("wait_sends")
     for copies in (edges5, edges4, edges3, edges2):
         for copy in copies:
             copy.wait_send()
-    pl.loop(0, peers)(lambda k: copyA(k).wait_send())
-    pl.loop(0, peers)(lambda k: copyB(k).wait_send())
+    pltpu.make_async_copy(recvA, recvA, all_send.at[0]).wait()
+    pltpu.make_async_copy(recvB, recvB, all_send.at[1]).wait()
+    phase("wait_B")
+    pltpu.make_async_copy(recvB, recvB, all_recv.at[1]).wait()
+    phase("normB")
+    totals = sendB[...] + jnp.sum(recvB[...], axis=0)
+    finish(1, totals)
+    phase(None)
+
+
+def write_out(*refs):
+    sems = refs[8]
+    copies = [pltpu.make_async_copy(refs[k], refs[4 + k], sems.at[k]) for k in range(4)]
+    for copy in copies:
+        copy.start()
+    for copy in copies:
+        copy.wait()
 
 
 def solution(mesh):
@@ -434,8 +496,8 @@
             vmem((1024, 256), BF16), vmem((2048, 256), BF16),
             vmem((4, 256), F32), vmem((4, 3, 768, 256), BF16),
             vmem((4, 256), F32), vmem((4, 256), F32),
-            vmem((2, 10, 256, 768), BF16), vmem((2, 6, 128, 768), BF16),
-            vmem((2, 4, 64, 768), BF16), vmem((2, 3, 32, 768), BF16),
+            vmem((2, 10, 6, 256, 128), BF16), vmem((2, 6, 6, 128, 128), BF16),
+            vmem((2, 4, 6, 64, 128), BF16), vmem((2, 3, 6, 32, 128), BF16),
             vmem((1536, 256), BF16), vmem((768, 256), BF16), vmem((256, 128), BF16),
             vmem((2, 512, 256), F32), vmem((2, 2, 64, 256), F32),
             vmem((2, 32, 256), BF16), vmem((2, 2, 64, 256), BF16), vmem((2, 2, 128, 256), BF16),
@@ -446,11 +508,11 @@
             vmem((2, 2048, 256), F32), vmem((2, 512, 256), F32),
             vmem((256, 256), F32), vmem((64, 256), F32),
             vmem((4, 2, 2, 8, 256), F32),
-            vmem((2, 128), F32), vmem((4, 128), F32),
-            vmem((strips - 1, 2, 128), F32), vmem((strips - 1, 4, 128), F32),
+            vmem((4, 128), F32), vmem((1, 128), F32),
+            vmem((strips - 1, 4, 128), F32), vmem((strips - 1, 1, 128), F32),
             pltpu.SemaphoreType.DMA((15,)),
             pltpu.SemaphoreType.DMA((4, 2)), pltpu.SemaphoreType.DMA((4, 2)),
-            pltpu.SemaphoreType.DMA((2, strips - 1)), pltpu.SemaphoreType.DMA((2, strips - 1)),
+            pltpu.SemaphoreType.DMA((2,)), pltpu.SemaphoreType.DMA((2,)),
         ]
         results = pl.pallas_call(
             lambda *refs: kernel(strips, *refs),
@@ -468,7 +530,19 @@
                 flops=7_430_000_000, bytes_accessed=13_300_000, transcendentals=0
             ),
         )(*(pltpu.with_memory_space_constraint(a, pltpu.HBM) for a in args))
-        return tuple(results)
+        return tuple(
+            pl.pallas_call(
+                write_out,
+                name="write",
+                out_shape=[jax.ShapeDtypeStruct(r.shape, r.dtype) for r in results],
+                in_specs=[pl.BlockSpec(memory_space=pltpu.VMEM)] * 4,
+                out_specs=[pl.BlockSpec(memory_space=pltpu.HBM)] * 4,
+                scratch_shapes=[pltpu.SemaphoreType.DMA((4,))],
+                cost_estimate=pl.CostEstimate(
+                    flops=0, bytes_accessed=5_600_000, transcendentals=0
+                ),
+            )(*(pltpu.with_memory_space_constraint(r, pltpu.VMEM) for r in results))
+        )
 
     rows = P("batch", "rows", None, None)
     return jax.shard_map(

time: 35.9 us -> 29.8 us (0.83)
  local copies, waits for them, and re-layouts: 3.38 us -> 0 us
  Pallas kernels: 31.8 us -> 29.1 us
    pallas_call x1, Pallas kernels: 31.8 us -> 27.5 us  [per_device(): pl.pallas_call(lambda *refs: kernel(strips, *refs), name='pyramid', out_s...]
    unnamed x4 -> x0, local copies, waits for them, and re-layouts: 3.38 us -> none
    pallas_call x0 -> x1, Pallas kernels: none -> 1.56 us  [per_device(): pl.pallas_call(write_out, name='write', out_shape=[jax.ShapeDtypeStruct(r...]
where the time goes in v2:
time: 29.8 us; the launch traced here: 29.7 us
  Pallas kernels  29.1 us (98%)
  between operations  0.64 us (2%)
    pallas_call x1, Pallas kernels, per_device(): pl.pallas_call(lambda *refs: kernel(strips, *refs), name='pyramid', out_s...  27.5 us
    pallas_call x1, Pallas kernels, per_device(): pl.pallas_call(write_out, name='write', out_shape=[jax.ShapeDtypeStruct(r...  1.56 us

profile of v2, /device:TPU:1, one launch (start us, length us, event | category | flops | bytes accessed | tf_op | source)
XLA Modules:
  0.0 29.7 jit_solution(17894560092629590855)
XLA Ops:
  0.6 27.5 %pyramid.1 = (bf16[2,8,256,256]{3,2,1,0:T(8,128)(2,1)S(1)}, bf16[2,4,128,256]{3,2,1,0:T(8,128)(2,1)S(1)}, bf16[2,2,64,256]{3,2,1,0:T(8,128)(2,1)S(1)}, bf16[2,1,32,256]{3,2,1,0:T(8,128)(2,1)S(1)}) custom-call(bf16[2,8,256,256]{3,2,1,0:T(8,128)(2,1)} %refs_0_.1, bf16[2,4,128,512]{3,2,1,0:T(8,128)(2,1)} %refs_1_.1, bf16[2,2,64,1024]{3,2,1,0:T(8,128)(2,1)} %refs_2_.1, ...), custom_call_target="tpu_custom_call" | custom-call | flops 7430000128 | bytes 13300000 | tf_op jit(solution)/shard_map/pyramid/pallas_call | solution.py:517
  28.2 1.6 %write.1 = (bf16[2,8,256,256]{3,2,1,0:T(8,128)(2,1)}, bf16[2,4,128,256]{3,2,1,0:T(8,128)(2,1)}, bf16[2,2,64,256]{3,2,1,0:T(8,128)(2,1)}, bf16[2,1,32,256]{3,2,1,0:T(8,128)(2,1)}) custom-call(bf16[2,8,256,256]{3,2,1,0:T(8,128)(2,1)S(1)} %get-tuple-element.8.refs_0_, bf16[2,4,128,256]{3,2,1,0:T(8,128)(2,1)S(1)} %get-tuple-element.9.refs_1_, ...), custom_call_target="tpu_custom_call" | custom-call | bytes 5600000 | tf_op jit(solution)/shard_map/write/pallas_call | solution.py:534

commit v3 on v2

--- a/solution.py
+++ b/solution.py
@@ -15,6 +15,7 @@
 COLS = (256, 128, 64, 32)
 STRIP = (8, 4, 2, 1)
 DEPTH = (256, 512, 1024, 2048)
+SIDE = 4
 
 
 def interpolation(cols, coarse_rows, pieces, width):
@@ -67,9 +68,26 @@
     return [(row(2 * image), row(2 * image + 1)) for image in range(IMAGES)]
 
 
+def affine_of(level, strips, totals, gain, offset):
+    entries = float(COLS[level] * strips * STRIP[level] * GROUP)
+    result = []
+    for sums, squares in decode(totals):
+        mean = sums / entries
+        variance = squares / entries - mean * mean
+        result.append((mean, lax.rsqrt(variance + EPSILON) * gain, offset))
+    return result
+
+
+def normalized(values, terms):
+    mean, scale, offset = terms
+    return ((values - mean) * scale + offset).astype(BF16)
+
+
 def kernel(strips, *refs):
     (f2, f3, f4, f5, w2, w3, w4, w5, bias, smooth, gain, shift) = refs[:12]
-    outs = refs[12:16]
+    outs = {0: refs[12], 2: refs[13], 3: refs[14], 4: refs[16]}
+    cv3 = refs[15]
+    norms = refs[17]
     (
         f2v, f3v, f4v, f5v, w2v, w3v, w4v, w5v, biasv, smv, gainv, shiftv,
         xc2, xc3, xc4, xc5,
@@ -78,11 +96,11 @@
         e5, e4, e3,
         r5, r4, r3, r2,
         rb2, rb3, rb4, rb5,
-        cv2, cv3, cv4, cv5,
+        cv2, cv4, cv5,
         stats,
         sendA, sendB, recvA, recvB,
-        in_sem, edge_send, edge_recv, all_send, all_recv,
-    ) = refs[16:]
+        in_sem, edge_send, edge_recv, all_send, all_recv, entered,
+    ) = refs[18:]
     current = []
 
     def phase(name):
@@ -99,12 +117,6 @@
     above = lax.rem(me + strips - 1, strips)
     below = lax.rem(me + 1, strips)
 
-    barrier = pltpu.get_barrier_semaphore()
-    for k in [1, strips - 1] + list(range(2, strips - 1)):
-        pl.semaphore_signal(
-            barrier, inc=1, device_id=(batch, lax.rem(me + k, strips)), device_id_type=MESH
-        )
-
     pairs = (
         (f5, f5v), (w5, w5v), (bias, biasv), (f4, f4v), (w4, w4v), (f3, f3v), (w3, w3v),
         (f2, f2v), (w2, w2v), (smooth.at[0], smv.at[0]), (smooth.at[1], smv.at[1]),
@@ -114,6 +126,30 @@
     for load in loads:
         load.start()
     (lf5, lw5, lb, lf4, lw4, lf3, lw3, lf2, lw2, ls2, ls3, ls4, ls5, lg, lsh) = loads
+
+    barrier = pltpu.get_barrier_semaphore()
+    core = lax.rem(me, 2)
+    x = lax.rem(lax.div(me, 2), SIDE)
+    y = lax.div(me, 2 * SIDE)
+    line = [
+        (y * SIDE + lax.rem(x + i, SIDE)) * 2 + lax.rem(core + c, 2)
+        for i in (0, 1, SIDE - 1, *range(2, SIDE - 1))
+        for c in range(2)
+        if i or c
+    ]
+    column = [(lax.rem(y + i, SIDE) * SIDE + x) * 2 + core for i in range(1, SIDE)]
+    ends_line = jnp.logical_and(lax.rem(me, 2 * SIDE) == 2 * SIDE - 1, me < strips - 1)
+    opens_line = jnp.logical_and(lax.rem(me, 2 * SIDE) == 0, me > 0)
+    has_above = me > 0
+    has_below = me < strips - 1
+
+    def greet(semaphore, peer):
+        pl.semaphore_signal(semaphore, inc=1, device_id=(batch, peer), device_id_type=MESH)
+
+    pl.when(ends_line)(lambda: greet(barrier, below))
+    pl.when(opens_line)(lambda: greet(barrier, above))
+    for peer in line + column:
+        greet(barrier, peer)
 
     first = me == 0
     last = me == strips - 1
@@ -175,8 +211,9 @@
         cols = values.shape[0]
         for half in range(2):
             rb[copy, half, 8 : 8 + cols, :] = values[:, 128 * half : 128 * half + 128]
-        for tap in range(3):
-            for half in range(2):
+        for half in range(2):
+            target[2 + half] = values[:, 128 * half : 128 * half + 128].astype(BF16)
+            for tap in (0, 2):
                 target[2 * tap + half] = rb[copy, half, 7 + tap : 7 + tap + cols, :].astype(BF16)
 
     def middle(xc, image, row, rows):
@@ -204,33 +241,59 @@
         edge(0, 1, f2v.at[:, 7], r2.at[0], below),
     )
 
-    phase("wait_load5")
+    def send(*levels):
+        @pl.when(has_above)
+        def _():
+            for pair_of in levels:
+                pair_of[0].start()
+
+        @pl.when(has_below)
+        def _():
+            for pair_of in levels:
+                pair_of[1].start()
+
+    def receive(*levels):
+        @pl.when(has_below)
+        def _():
+            for pair_of in levels:
+                pair_of[0].wait_recv()
+
+        @pl.when(has_above)
+        def _():
+            for pair_of in levels:
+                pair_of[1].wait_recv()
+
+    for side, missing in ((0, first), (1, last)):
+
+        @pl.when(missing)
+        def _():
+            for halo in (r5, r4, r3, r2):
+                halo[side] = jnp.zeros_like(halo[side])
+
+    phase("wait_load54")
     lf5.wait()
     lw5.wait()
     lb.wait()
-    phase("lat5")
+    lf4.wait()
+    lw4.wait()
+    phase("lat54")
     merged = dot(f5v[...].reshape(64, 2048), w5v[...]) + biasv[3:4, :]
     e5[...] = merged.reshape(2, 32, 256).astype(BF16)
-    phase("barrier")
-    pl.semaphore_wait(barrier, peers)
-    phase("put5")
+    flat = dot(f4v[...].reshape(256, 1024), w4v[...]) + biasv[2:3, :]
     for image in range(IMAGES):
         put_row(rb5, image, xc5.at[image, 1], merged[32 * image : 32 * image + 32])
-    for copy in edges5:
-        copy.start()
-
-    phase("wait_load4")
-    lf4.wait()
-    lw4.wait()
-    phase("lat4")
-    flat = dot(f4v[...].reshape(256, 1024), w4v[...]) + biasv[2:3, :]
-    for image in range(IMAGES):
         for row in range(2):
             part = flat[(2 * image + row) * 64 : (2 * image + row) * 64 + 64]
             e4[row, image] = part.astype(BF16)
             lat4[image, row] = part
-    for copy in edges4:
-        copy.start()
+    phase("barrier")
+    pl.semaphore_wait(
+        barrier,
+        len(line + column) + jnp.where(jnp.logical_or(ends_line, opens_line), 1, 0),
+    )
+    send(edges5, edges4)
+    for peer in column:
+        greet(entered, peer)
 
     phase("wait_load3")
     lf3.wait()
@@ -241,12 +304,10 @@
         e3[0, image] = flat[0:128].astype(BF16)
         e3[1, image] = flat[384:512].astype(BF16)
         lat3[image] = flat
-    for copy in edges3:
-        copy.start()
+    send(edges3)
     phase("wait_load2")
     lf2.wait()
-    for copy in edges2:
-        copy.start()
+    send(edges2)
 
     phase("lat2")
     lw2.wait()
@@ -258,48 +319,39 @@
                 dot(f2v[image, 4 * part : 4 * part + 4].reshape(1024, 256), w2v[...])
                 + biasv[0:1, :]
             )
+    ls2.wait()
 
     phase("wait_edge5")
-    for copy in edges5:
-        copy.wait_recv()
-    phase("halo5")
-    for image in range(IMAGES):
-        put_row(rb5, image, xc5.at[image, 0], r5[0, image].astype(F32) * keep_top)
-        put_row(rb5, 2 + image, xc5.at[image, 2], r5[1, image].astype(F32) * keep_bottom)
-    phase("wait_edge4")
-    for copy in edges4:
-        copy.wait_recv()
-    phase("merge4")
+    receive(edges5, edges4)
+    phase("merge")
+    for image in range(IMAGES):
+        put_row(rb5, 2 + image, xc5.at[image, 0], r5[0, image].astype(F32) * keep_top)
+        put_row(rb5, 4 + image, xc5.at[image, 2], r5[1, image].astype(F32) * keep_bottom)
     for image in range(IMAGES):
         coarse = jnp.concatenate(
             [middle(xc5, image, 0, 3), jnp.zeros((32, 256), BF16)], 0
         )
         up = dot(t4[...], coarse)
-        put_row(rb4, 0, xc4.at[image, 0], (up[0:64] + r4[0, image].astype(F32)) * keep_top)
-        put_row(rb4, 1, xc4.at[image, 1], up[64:128] + lat4[image, 0])
-        put_row(rb4, 2, xc4.at[image, 2], up[128:192] + lat4[image, 1])
-        put_row(rb4, 3, xc4.at[image, 3], (up[192:256] + r4[1, image].astype(F32)) * keep_bottom)
-
-    phase("merge3")
+        put_row(rb4, 4 * image + 0, xc4.at[image, 0], (up[0:64] + r4[0, image].astype(F32)) * keep_top)
+        put_row(rb4, 4 * image + 1, xc4.at[image, 1], up[64:128] + lat4[image, 0])
+        put_row(rb4, 4 * image + 2, xc4.at[image, 2], up[128:192] + lat4[image, 1])
+        put_row(rb4, 4 * image + 3, xc4.at[image, 3], (up[192:256] + r4[1, image].astype(F32)) * keep_bottom)
+
     for image in range(IMAGES):
         up = dot(t3[0:512, :], middle(xc4, image, 0, 4)) + lat3[image]
         for row in range(4):
-            put_row(rb3, row, xc3.at[image, 1 + row], up[128 * row : 128 * row + 128])
-
-    phase("wait_w2")
+            put_row(rb3, 4 * image + row, xc3.at[image, 1 + row], up[128 * row : 128 * row + 128])
 
     def pair(image, p, weights):
         return dot(weights, middle(xc3, image, p + 1, 2))
 
-    phase("merge2")
-    @pl.loop(0, IMAGES)
-    def _(image):
+    def merge_middle(image):
         for p in range(3):
             both = pair(image, p, t2[0:512, :])
             for row in range(2):
                 start = 512 * p + 256 + 256 * row
                 put_row(
-                    rb2, row, xc2.at[image, 2 * p + 2 + row],
+                    rb2, 6 * image + 2 * p + row, xc2.at[image, 2 * p + 2 + row],
                     both[256 * row : 256 * row + 256] + cv2[image, start : start + 256, :],
                 )
 
@@ -324,53 +376,41 @@
             level,
         )
 
-    phase("wait_s2")
-    ls2.wait()
-
     def conv_two(image, row):
         values = conv(xc2, 0, image, row, 2)
         cv2[image, row * 256 : row * 256 + 512, :] = values
         tally(0, image, values)
 
-    phase("conv2a")
-    @pl.loop(0, IMAGES)
-    def _(image):
+    for image in range(IMAGES):
+        merge_middle(image)
         for row in (2, 4):
             conv_two(image, row)
 
     phase("wait_edge3")
-    for copy in edges3:
-        copy.wait_recv()
-    phase("halo3")
+    receive(edges3, edges2)
+    ls4.wait()
+    ls5.wait()
+    phase("rest2")
     for image in range(IMAGES):
         up = dot(t3[512:768, :], middle(xc4, image, 0, 4))
-        put_row(rb3, 0, xc3.at[image, 0], (up[0:128] + r3[0, image].astype(F32)) * keep_top)
-        put_row(rb3, 1, xc3.at[image, 5], (up[128:256] + r3[1, image].astype(F32)) * keep_bottom)
-    phase("wait_edge2")
-    for copy in edges2:
-        copy.wait_recv()
-
-    phase("merge2b")
-    @pl.loop(0, IMAGES)
-    def _(image):
+        put_row(rb3, 8 + image, xc3.at[image, 0], (up[0:128] + r3[0, image].astype(F32)) * keep_top)
+        put_row(rb3, 10 + image, xc3.at[image, 5], (up[128:256] + r3[1, image].astype(F32)) * keep_bottom)
+    def merge_ends(image):
         both = pair(image, -1, t2[512:1024, :])
         outside = dot(r2[0, image], w2v[...]) + biasv[0:1, :]
-        put_row(rb2, 0, xc2.at[image, 0], (both[0:256] + outside) * keep_top)
-        put_row(rb2, 1, xc2.at[image, 1], both[256:512] + cv2[image, 0:256, :])
+        base = 12 + 4 * image
+        put_row(rb2, base, xc2.at[image, 0], (both[0:256] + outside) * keep_top)
+        put_row(rb2, base + 1, xc2.at[image, 1], both[256:512] + cv2[image, 0:256, :])
         both = pair(image, 3, t2[1024:1536, :])
         outside = dot(r2[1, image], w2v[...]) + biasv[0:1, :]
-        put_row(rb2, 2, xc2.at[image, 8], both[0:256] + cv2[image, 1792:2048, :])
-        put_row(rb2, 3, xc2.at[image, 9], (both[256:512] + outside) * keep_bottom)
-
-    phase("conv2b")
-    @pl.loop(0, IMAGES)
-    def _(image):
+        put_row(rb2, base + 2, xc2.at[image, 8], both[0:256] + cv2[image, 1792:2048, :])
+        put_row(rb2, base + 3, xc2.at[image, 9], (both[256:512] + outside) * keep_bottom)
+
+    for image in range(IMAGES):
+        merge_ends(image)
         for row in (0, 6):
             conv_two(image, row)
 
-    phase("conv54")
-    ls4.wait()
-    ls5.wait()
     values = product(
         [[xc5[:, tap, slab].reshape(64, 128) for slab in range(6)] for tap in range(3)], 3
     )
@@ -405,6 +445,7 @@
     sendA[...] = jnp.concatenate(
         [encode(stats.at[0]), encode(stats.at[2]), encode(stats.at[3]), jnp.zeros((1, 128), F32)], 0
     )
+    pl.semaphore_wait(entered, len(column))
     for copy in everyone(sendA, recvA, 0):
         copy.start()
 
@@ -420,22 +461,13 @@
     for copy in everyone(sendB, recvB, 1):
         copy.start()
 
-    def affine(level, sums, squares):
-        entries = float(COLS[level] * strips * STRIP[level] * GROUP)
-        mean = sums / entries
-        variance = squares / entries - mean * mean
-        scale = lax.rsqrt(variance + EPSILON) * gainv[level : level + 1, :]
-        return mean, scale, shiftv[level : level + 1, :]
-
-    def normalized(values, terms):
-        mean, scale, offset = terms
-        return ((values - mean) * scale + offset).astype(BF16)
-
     lg.wait()
     lsh.wait()
+    norms[0:1, :] = gainv[1:2, :]
+    norms[1:2, :] = shiftv[1:2, :]
     def finish(level, totals):
-        for image, (sums, squares) in enumerate(decode(totals)):
-            terms = affine(level, sums, squares)
+        affine = affine_of(level, strips, totals, gainv[level : level + 1], shiftv[level : level + 1])
+        for image, terms in enumerate(affine):
             if level == 0:
 
                 @pl.loop(0, 8)
@@ -443,9 +475,7 @@
                     outs[0][image, row] = normalized(cv2[image, pl.ds(row * 256, 256), :], terms)
 
                 continue
-            if level == 1:
-                values = cv3[image]
-            elif level == 2:
+            if level == 2:
                 values = cv4[128 * image : 128 * image + 128]
             else:
                 values = cv5[32 * image : 32 * image + 32]
@@ -462,24 +492,38 @@
     finish(3, totals[2:3])
 
     phase("wait_sends")
-    for copies in (edges5, edges4, edges3, edges2):
-        for copy in copies:
-            copy.wait_send()
+    @pl.when(has_above)
+    def _():
+        for pair_of in (edges5, edges4, edges3, edges2):
+            pair_of[0].wait_send()
+
+    @pl.when(has_below)
+    def _():
+        for pair_of in (edges5, edges4, edges3, edges2):
+            pair_of[1].wait_send()
+
     pltpu.make_async_copy(recvA, recvA, all_send.at[0]).wait()
     pltpu.make_async_copy(recvB, recvB, all_send.at[1]).wait()
     phase("wait_B")
     pltpu.make_async_copy(recvB, recvB, all_recv.at[1]).wait()
     phase("normB")
-    totals = sendB[...] + jnp.sum(recvB[...], axis=0)
-    finish(1, totals)
+    outs[4][...] = sendB[...] + jnp.sum(recvB[...], axis=0)
     phase(None)
 
 
-def write_out(*refs):
-    sems = refs[8]
-    copies = [pltpu.make_async_copy(refs[k], refs[4 + k], sems.at[k]) for k in range(4)]
-    for copy in copies:
+def write_out(strips, in2, in4, in5, values, totals, norms, out2, out3, out4, out5, made3, sems):
+    copies = [
+        pltpu.make_async_copy(source, target, sems.at[k])
+        for k, (source, target) in enumerate(
+            ((in2, out2), (in4, out4), (in5, out5), (made3, out3))
+        )
+    ]
+    for copy in copies[:3]:
         copy.start()
+    affine = affine_of(1, strips, totals[...], norms[0:1, :], norms[1:2, :])
+    for image, terms in enumerate(affine):
+        made3[image] = normalized(values[image], terms).reshape(STRIP[1], COLS[1], CHANNELS)
+    copies[3].start()
     for copy in copies:
         copy.wait()
 
@@ -503,25 +547,30 @@
             vmem((2, 32, 256), BF16), vmem((2, 2, 64, 256), BF16), vmem((2, 2, 128, 256), BF16),
             vmem((2, 2, 32, 256), BF16), vmem((2, 2, 64, 256), BF16),
             vmem((2, 2, 128, 256), BF16), vmem((2, 2, 256, 256), BF16),
-            vmem((4, 2, 272, 128), F32), vmem((4, 2, 144, 128), F32),
-            vmem((4, 2, 80, 128), F32), vmem((4, 2, 48, 128), F32),
-            vmem((2, 2048, 256), F32), vmem((2, 512, 256), F32),
-            vmem((256, 256), F32), vmem((64, 256), F32),
+            vmem((20, 2, 272, 128), F32), vmem((12, 2, 144, 128), F32),
+            vmem((8, 2, 80, 128), F32), vmem((6, 2, 48, 128), F32),
+            vmem((2, 2048, 256), F32), vmem((256, 256), F32), vmem((64, 256), F32),
             vmem((4, 2, 2, 8, 256), F32),
             vmem((4, 128), F32), vmem((1, 128), F32),
             vmem((strips - 1, 4, 128), F32), vmem((strips - 1, 1, 128), F32),
             pltpu.SemaphoreType.DMA((15,)),
             pltpu.SemaphoreType.DMA((4, 2)), pltpu.SemaphoreType.DMA((4, 2)),
             pltpu.SemaphoreType.DMA((2,)), pltpu.SemaphoreType.DMA((2,)),
+            pltpu.SemaphoreType.REGULAR,
         ]
         results = pl.pallas_call(
             lambda *refs: kernel(strips, *refs),
             name="pyramid",
             out_shape=[
-                pltpu.VMEM((IMAGES, STRIP[k], COLS[k], CHANNELS), BF16) for k in range(4)
+                pltpu.VMEM((IMAGES, STRIP[k], COLS[k], CHANNELS), BF16) for k in (0, 2, 3)
+            ]
+            + [
+                pltpu.VMEM((IMAGES, STRIP[1] * COLS[1], CHANNELS), F32),
+                pltpu.VMEM((1, 128), F32),
+                pltpu.VMEM((2, CHANNELS), F32),
             ],
             in_specs=[pl.BlockSpec(memory_space=pltpu.HBM)] * 12,
-            out_specs=[pl.BlockSpec(memory_space=pltpu.VMEM)] * 4,
+            out_specs=[pl.BlockSpec(memory_space=pltpu.VMEM)] * 6,
             scratch_shapes=scratch,
             compiler_params=pltpu.CompilerParams(
                 collective_id=0, has_side_effects=True, vmem_limit_bytes=48 << 20
@@ -532,12 +581,18 @@
         )(*(pltpu.with_memory_space_constraint(a, pltpu.HBM) for a in args))
         return tuple(
             pl.pallas_call(
-                write_out,
+                lambda *refs: write_out(strips, *refs),
                 name="write",
-                out_shape=[jax.ShapeDtypeStruct(r.shape, r.dtype) for r in results],
-                in_specs=[pl.BlockSpec(memory_space=pltpu.VMEM)] * 4,
+                out_shape=[
+                    jax.ShapeDtypeStruct((IMAGES, STRIP[k], COLS[k], CHANNELS), BF16)
+                    for k in range(4)
+                ],
+                in_specs=[pl.BlockSpec(memory_space=pltpu.VMEM)] * 6,
                 out_specs=[pl.BlockSpec(memory_space=pltpu.HBM)] * 4,
-                scratch_shapes=[pltpu.SemaphoreType.DMA((4,))],
+                scratch_shapes=[
+                    pltpu.VMEM((IMAGES, STRIP[1], COLS[1], CHANNELS), BF16),
+                    pltpu.SemaphoreType.DMA((4,)),
+                ],
                 cost_estimate=pl.CostEstimate(
                     flops=0, bytes_accessed=5_600_000, transcendentals=0
                 ),

time: 29.8 us -> 26.8 us (0.90)
  Pallas kernels: 29.1 us -> 26.1 us
    pallas_call x1, Pallas kernels: 27.5 us -> 24.5 us  [per_device(): pl.pallas_call(lambda *refs: kernel(strips, *refs), name='pyramid', out_s...]
where the time goes in v3:
time: 26.8 us; the launch traced here: 26.7 us
  Pallas kernels  26.1 us (97%)
  between operations  0.64 us (2%)
    pallas_call x1, Pallas kernels, per_device(): pl.pallas_call(lambda *refs: kernel(strips, *refs), name='pyramid', out_s...  24.5 us
    pallas_call x1, Pallas kernels, per_device(): pl.pallas_call(lambda *refs: write_out(strips, *refs), name='write', out_...  1.58 us

profile of v3, /device:TPU:1, one launch (start us, length us, event | category | flops | bytes accessed | tf_op | source)
XLA Modules:
  0.0 26.7 jit_solution(16635290929736919761)
XLA Ops:
  0.6 24.5 %pyramid.1 = (bf16[2,8,256,256]{3,2,1,0:T(8,128)(2,1)S(1)}, bf16[2,2,64,256]{3,2,1,0:T(8,128)(2,1)S(1)}, bf16[2,1,32,256]{3,2,1,0:T(8,128)(2,1)S(1)}, f32[2,512,...) custom-call(bf16[2,8,256,256]{3,2,1,0:T(8,128)(2,1)} %refs_0_.1, bf16[2,4,128,512]{3,2,1,0:T(8,128)(2,1)} %refs_1_.1, ...), custom_call_target="tpu_custom_call" | custom-call | flops 7430000128 | bytes 13300000 | tf_op jit(solution)/shard_map/pyramid/pallas_call | solution.py:561
  25.1 1.6 %write.1 = (bf16[2,8,256,256]{3,2,1,0:T(8,128)(2,1)}, bf16[2,4,128,256]{3,2,1,0:T(8,128)(2,1)}, bf16[2,2,64,256]{3,2,1,0:T(8,128)(2,1)}, bf16[2,1,32,256]{3,2,1,0:T(8,128)(2,1)}) custom-call(bf16[2,8,256,256]{3,2,1,0:T(8,128)(2,1)S(1)} %get-tuple-element.10.refs_0_, bf16[2,2,64,256]{3,2,1,0:T(8,128)(2,1)S(1)} %get-tuple-element.11.refs_1_, ...), custom_call_target="tpu_custom_call" | custom-call | bytes 5600000 | tf_op jit(solution)/shard_map/write/pallas_call | solution.py:583

commit v4 on v3

--- a/solution.py
+++ b/solution.py
@@ -68,26 +68,28 @@
     return [(row(2 * image), row(2 * image + 1)) for image in range(IMAGES)]
 
 
-def affine_of(level, strips, totals, gain, offset):
+def affine_of(level, strips, totals, gain, shift):
     entries = float(COLS[level] * strips * STRIP[level] * GROUP)
     result = []
     for sums, squares in decode(totals):
         mean = sums / entries
         variance = squares / entries - mean * mean
-        result.append((mean, lax.rsqrt(variance + EPSILON) * gain, offset))
+        factor = lax.rsqrt(variance + EPSILON) * gain
+        result.append((factor, shift - mean * factor))
     return result
 
 
 def normalized(values, terms):
-    mean, scale, offset = terms
-    return ((values - mean) * scale + offset).astype(BF16)
-
-
-def kernel(strips, *refs):
+    factor, offset = terms
+    return (values * factor + offset).astype(BF16)
+
+
+def kernel(strips, refs, in_sem):
     (f2, f3, f4, f5, w2, w3, w4, w5, bias, smooth, gain, shift) = refs[:12]
     outs = {0: refs[12], 2: refs[13], 3: refs[14], 4: refs[16]}
     cv3 = refs[15]
     norms = refs[17]
+    cv2 = refs[18]
     (
         f2v, f3v, f4v, f5v, w2v, w3v, w4v, w5v, biasv, smv, gainv, shiftv,
         xc2, xc3, xc4, xc5,
@@ -96,11 +98,11 @@
         e5, e4, e3,
         r5, r4, r3, r2,
         rb2, rb3, rb4, rb5,
-        cv2, cv4, cv5,
+        cv4, cv5,
         stats,
         sendA, sendB, recvA, recvB,
-        in_sem, edge_send, edge_recv, all_send, all_recv, entered,
-    ) = refs[18:]
+        edge_send, edge_recv, all_send, all_recv, entered,
+    ) = refs[19:]
     current = []
 
     def phase(name):
@@ -118,37 +120,33 @@
     below = lax.rem(me + 1, strips)
 
     pairs = (
-        (f5, f5v), (w5, w5v), (bias, biasv), (f4, f4v), (w4, w4v), (f3, f3v), (w3, w3v),
+        (f4, f4v), (w4, w4v), (bias, biasv), (f5, f5v), (w5, w5v), (f3, f3v), (w3, w3v),
         (f2, f2v), (w2, w2v), (smooth.at[0], smv.at[0]), (smooth.at[1], smv.at[1]),
         (smooth.at[2], smv.at[2]), (smooth.at[3], smv.at[3]), (gain, gainv), (shift, shiftv),
     )
     loads = [pltpu.make_async_copy(s, d, in_sem.at[i]) for i, (s, d) in enumerate(pairs)]
     for load in loads:
         load.start()
-    (lf5, lw5, lb, lf4, lw4, lf3, lw3, lf2, lw2, ls2, ls3, ls4, ls5, lg, lsh) = loads
+    (lf4, lw4, lb, lf5, lw5, lf3, lw3, lf2, lw2, ls2, ls3, ls4, ls5, lg, lsh) = loads
 
     barrier = pltpu.get_barrier_semaphore()
     core = lax.rem(me, 2)
     x = lax.rem(lax.div(me, 2), SIDE)
     y = lax.div(me, 2 * SIDE)
-    line = [
-        (y * SIDE + lax.rem(x + i, SIDE)) * 2 + lax.rem(core + c, 2)
-        for i in (0, 1, SIDE - 1, *range(2, SIDE - 1))
-        for c in range(2)
-        if i or c
-    ]
-    column = [(lax.rem(y + i, SIDE) * SIDE + x) * 2 + core for i in range(1, SIDE)]
-    ends_line = jnp.logical_and(lax.rem(me, 2 * SIDE) == 2 * SIDE - 1, me < strips - 1)
-    opens_line = jnp.logical_and(lax.rem(me, 2 * SIDE) == 0, me > 0)
+    place = lambda j, i, c: (lax.rem(y + j, SIDE) * SIDE + lax.rem(x + i, SIDE)) * 2 + c
+    partner = me + 1 - 2 * core
+    nearest = [place(0, 1, core), place(0, SIDE - 1, core), place(1, 0, core), place(SIDE - 1, 0, core)]
+    line = [place(0, i, core) for i in range(1, SIDE)]
+    side = me + 2 * core - 1
+    has_side = jnp.logical_and(side >= 0, side < strips)
     has_above = me > 0
     has_below = me < strips - 1
 
     def greet(semaphore, peer):
         pl.semaphore_signal(semaphore, inc=1, device_id=(batch, peer), device_id_type=MESH)
 
-    pl.when(ends_line)(lambda: greet(barrier, below))
-    pl.when(opens_line)(lambda: greet(barrier, above))
-    for peer in line + column:
+    pl.when(has_side)(lambda: greet(barrier, side))
+    for peer in nearest + [partner]:
         greet(barrier, peer)
 
     first = me == 0
@@ -270,30 +268,31 @@
             for halo in (r5, r4, r3, r2):
                 halo[side] = jnp.zeros_like(halo[side])
 
-    phase("wait_load54")
-    lf5.wait()
-    lw5.wait()
-    lb.wait()
+    phase("wait_load4")
     lf4.wait()
     lw4.wait()
-    phase("lat54")
-    merged = dot(f5v[...].reshape(64, 2048), w5v[...]) + biasv[3:4, :]
-    e5[...] = merged.reshape(2, 32, 256).astype(BF16)
-    flat = dot(f4v[...].reshape(256, 1024), w4v[...]) + biasv[2:3, :]
-    for image in range(IMAGES):
-        put_row(rb5, image, xc5.at[image, 1], merged[32 * image : 32 * image + 32])
+    lb.wait()
+    phase("lat4")
+    for image in range(IMAGES):
+        flat = dot(f4v[image].reshape(128, 1024), w4v[...]) + biasv[2:3, :]
         for row in range(2):
-            part = flat[(2 * image + row) * 64 : (2 * image + row) * 64 + 64]
+            part = flat[row * 64 : row * 64 + 64]
             e4[row, image] = part.astype(BF16)
             lat4[image, row] = part
     phase("barrier")
-    pl.semaphore_wait(
-        barrier,
-        len(line + column) + jnp.where(jnp.logical_or(ends_line, opens_line), 1, 0),
-    )
-    send(edges5, edges4)
-    for peer in column:
-        greet(entered, peer)
+    pl.semaphore_wait(barrier, 5 + jnp.where(has_side, 1, 0))
+    send(edges4)
+    phase("wait_load5")
+    lf5.wait()
+    lw5.wait()
+    phase("lat5")
+    merged = dot(f5v[...].reshape(64, 2048), w5v[...]) + biasv[3:4, :]
+    e5[...] = merged.reshape(2, 32, 256).astype(BF16)
+    for image in range(IMAGES):
+        put_row(rb5, image, xc5.at[image, 1], merged[32 * image : 32 * image + 32])
+    send(edges5)
+    for peer in nearest + [partner]:
+        greet(entered.at[0], peer)
 
     phase("wait_load3")
     lf3.wait()
@@ -320,30 +319,37 @@
                 + biasv[0:1, :]
             )
     ls2.wait()
+    ls4.wait()
+    ls5.wait()
 
     phase("wait_edge5")
     receive(edges5, edges4)
+    pl.semaphore_wait(entered.at[0], 5)
+    for peer in line:
+        greet(entered.at[1], peer)
     phase("merge")
-    for image in range(IMAGES):
+    def pair(image, p, weights):
+        return dot(weights, middle(xc3, image, p + 1, 2))
+
+    def halo_five(image):
         put_row(rb5, 2 + image, xc5.at[image, 0], r5[0, image].astype(F32) * keep_top)
         put_row(rb5, 4 + image, xc5.at[image, 2], r5[1, image].astype(F32) * keep_bottom)
-    for image in range(IMAGES):
-        coarse = jnp.concatenate(
-            [middle(xc5, image, 0, 3), jnp.zeros((32, 256), BF16)], 0
+
+    def merge_four(image):
+        coarse = jnp.concatenate([middle(xc5, image, 0, 3), jnp.zeros((32, 256), BF16)], 0)
+        up = dot(t4[...], coarse)
+        base = 4 * image
+        put_row(rb4, base, xc4.at[image, 0], (up[0:64] + r4[0, image].astype(F32)) * keep_top)
+        put_row(rb4, base + 1, xc4.at[image, 1], up[64:128] + lat4[image, 0])
+        put_row(rb4, base + 2, xc4.at[image, 2], up[128:192] + lat4[image, 1])
+        put_row(
+            rb4, base + 3, xc4.at[image, 3], (up[192:256] + r4[1, image].astype(F32)) * keep_bottom
         )
-        up = dot(t4[...], coarse)
-        put_row(rb4, 4 * image + 0, xc4.at[image, 0], (up[0:64] + r4[0, image].astype(F32)) * keep_top)
-        put_row(rb4, 4 * image + 1, xc4.at[image, 1], up[64:128] + lat4[image, 0])
-        put_row(rb4, 4 * image + 2, xc4.at[image, 2], up[128:192] + lat4[image, 1])
-        put_row(rb4, 4 * image + 3, xc4.at[image, 3], (up[192:256] + r4[1, image].astype(F32)) * keep_bottom)
-
-    for image in range(IMAGES):
+
+    def merge_three(image):
         up = dot(t3[0:512, :], middle(xc4, image, 0, 4)) + lat3[image]
         for row in range(4):
             put_row(rb3, 4 * image + row, xc3.at[image, 1 + row], up[128 * row : 128 * row + 128])
-
-    def pair(image, p, weights):
-        return dot(weights, middle(xc3, image, p + 1, 2))
 
     def merge_middle(image):
         for p in range(3):
@@ -381,15 +387,42 @@
         cv2[image, row * 256 : row * 256 + 512, :] = values
         tally(0, image, values)
 
+    for stage in (halo_five, merge_four, merge_three):
+        for image in range(IMAGES):
+            stage(image)
     for image in range(IMAGES):
         merge_middle(image)
         for row in (2, 4):
             conv_two(image, row)
 
+    values = product(
+        [[xc5[:, tap, slab].reshape(64, 128) for slab in range(6)] for tap in range(3)], 3
+    )
+    cv5[...] = values
+    for image in range(IMAGES):
+        tally(3, image, values[32 * image : 32 * image + 32])
+    values = product(
+        [
+            [xc4[:, tap : tap + 2, slab].reshape(256, 128) for slab in range(6)]
+            for tap in range(3)
+        ],
+        2,
+    )
+    cv4[...] = values
+    for image in range(IMAGES):
+        tally(2, image, values[128 * image : 128 * image + 128])
+
+    def conv_three(row, rows):
+        for image in range(IMAGES):
+            values = conv(xc3, 1, image, row, rows)
+            cv3[image, 128 * row : 128 * (row + rows)] = values
+            tally(1, image, values)
+
     phase("wait_edge3")
     receive(edges3, edges2)
-    ls4.wait()
-    ls5.wait()
+    pl.semaphore_wait(entered.at[1], 3)
+    greet(entered.at[2], partner)
+    ls3.wait()
     phase("rest2")
     for image in range(IMAGES):
         up = dot(t3[512:768, :], middle(xc4, image, 0, 4))
@@ -411,50 +444,40 @@
         for row in (0, 6):
             conv_two(image, row)
 
-    values = product(
-        [[xc5[:, tap, slab].reshape(64, 128) for slab in range(6)] for tap in range(3)], 3
-    )
-    cv5[...] = values
-    for image in range(IMAGES):
-        tally(3, image, values[32 * image : 32 * image + 32])
-    values = product(
-        [
-            [xc4[:, tap : tap + 2, slab].reshape(256, 128) for slab in range(6)]
-            for tap in range(3)
-        ],
-        2,
-    )
-    cv4[...] = values
-    for image in range(IMAGES):
-        tally(2, image, values[128 * image : 128 * image + 128])
+    conv_three(1, 2)
 
     def everyone(source, target, which):
+        far = lambda i: min(i, SIDE - i)
+        moves = sorted(
+            ((j, i, c) for j in range(SIDE) for i in range(SIDE) for c in range(2) if i or j or c),
+            key=lambda m: (-far(m[0]) - far(m[1]), m),
+        )
+        along = [2 * lax.rem(x + i, SIDE) for i in range(SIDE)]
+        across = [2 * SIDE * lax.rem(y + j, SIDE) for j in range(SIDE)]
+        cores = [core, 1 - core]
         return [
             pltpu.make_async_remote_copy(
                 src_ref=source,
-                dst_ref=target.at[k],
+                dst_ref=target.at[slot],
                 send_sem=all_send.at[which],
                 recv_sem=all_recv.at[which],
-                device_id=(batch, lax.rem(me + 1 + k, strips)),
+                device_id=(batch, across[j] + along[i] + cores[c]),
                 device_id_type=MESH,
             )
-            for k in range(peers)
+            for slot, (j, i, c) in enumerate(moves)
         ]
 
     phase("encodeA")
     sendA[...] = jnp.concatenate(
         [encode(stats.at[0]), encode(stats.at[2]), encode(stats.at[3]), jnp.zeros((1, 128), F32)], 0
     )
-    pl.semaphore_wait(entered, len(column))
+    pl.semaphore_wait(entered.at[2], 1)
     for copy in everyone(sendA, recvA, 0):
         copy.start()
 
     phase("conv3")
-    ls3.wait()
-    for image in range(IMAGES):
-        values = conv(xc3, 1, image, 0, 4)
-        cv3[image] = values
-        tally(1, image, values)
+    for row in (0, 3):
+        conv_three(row, 1)
 
     phase("encodeB")
     sendB[...] = encode(stats.at[1])
@@ -468,20 +491,23 @@
     def finish(level, totals):
         affine = affine_of(level, strips, totals, gainv[level : level + 1], shiftv[level : level + 1])
         for image, terms in enumerate(affine):
-            if level == 0:
-
-                @pl.loop(0, 8)
-                def _(row):
-                    outs[0][image, row] = normalized(cv2[image, pl.ds(row * 256, 256), :], terms)
-
-                continue
-            if level == 2:
-                values = cv4[128 * image : 128 * image + 128]
+            if level == 0 and image == 0:
+
+                @pl.loop(0, 4)
+                def _(rows):
+                    values = normalized(cv2[0, pl.ds(rows * 512, 512), :], terms)
+                    outs[0][0, pl.ds(rows * 2, 2)] = values.reshape(2, 256, 256)
+
+            elif level == 0:
+                norms[2:3, :], norms[3:4, :] = terms
             else:
-                values = cv5[32 * image : 32 * image + 32]
-            outs[level][image] = normalized(values, terms).reshape(
-                STRIP[level], COLS[level], 256
-            )
+                if level == 2:
+                    values = cv4[128 * image : 128 * image + 128]
+                else:
+                    values = cv5[32 * image : 32 * image + 32]
+                outs[level][image] = normalized(values, terms).reshape(
+                    STRIP[level], COLS[level], 256
+                )
 
     phase("wait_A")
     pltpu.make_async_copy(recvA, recvA, all_recv.at[0]).wait()
@@ -511,19 +537,24 @@
     phase(None)
 
 
-def write_out(strips, in2, in4, in5, values, totals, norms, out2, out3, out4, out5, made3, sems):
-    copies = [
-        pltpu.make_async_copy(source, target, sems.at[k])
-        for k, (source, target) in enumerate(
-            ((in2, out2), (in4, out4), (in5, out5), (made3, out3))
-        )
-    ]
+def write_out(
+    strips, in2, in4, in5, values, totals, norms, values2, out2, out3, out4, out5, made2, made3, sems
+):
+    pairs = [(in2, out2.at[pl.ds(0, 1)]), (in4, out4), (in5, out5)]
+    pairs += [(made2.at[pl.ds(4 * j, 4)], out2.at[1, pl.ds(4 * j, 4)]) for j in range(2)]
+    pairs += [(made3, out3)]
+    copies = [pltpu.make_async_copy(*pair, sems.at[k]) for k, pair in enumerate(pairs)]
     for copy in copies[:3]:
         copy.start()
+    terms = (norms[2:3, :], norms[3:4, :])
+    for j in range(2):
+        rows = normalized(values2[1, 1024 * j : 1024 * j + 1024, :], terms)
+        made2[4 * j : 4 * j + 4] = rows.reshape(4, COLS[0], CHANNELS)
+        copies[3 + j].start()
     affine = affine_of(1, strips, totals[...], norms[0:1, :], norms[1:2, :])
     for image, terms in enumerate(affine):
         made3[image] = normalized(values[image], terms).reshape(STRIP[1], COLS[1], CHANNELS)
-    copies[3].start()
+    copies[5].start()
     for copy in copies:
         copy.wait()
 
@@ -549,28 +580,31 @@
             vmem((2, 2, 128, 256), BF16), vmem((2, 2, 256, 256), BF16),
             vmem((20, 2, 272, 128), F32), vmem((12, 2, 144, 128), F32),
             vmem((8, 2, 80, 128), F32), vmem((6, 2, 48, 128), F32),
-            vmem((2, 2048, 256), F32), vmem((256, 256), F32), vmem((64, 256), F32),
+            vmem((256, 256), F32), vmem((64, 256), F32),
             vmem((4, 2, 2, 8, 256), F32),
             vmem((4, 128), F32), vmem((1, 128), F32),
             vmem((strips - 1, 4, 128), F32), vmem((strips - 1, 1, 128), F32),
-            pltpu.SemaphoreType.DMA((15,)),
             pltpu.SemaphoreType.DMA((4, 2)), pltpu.SemaphoreType.DMA((4, 2)),
             pltpu.SemaphoreType.DMA((2,)), pltpu.SemaphoreType.DMA((2,)),
-            pltpu.SemaphoreType.REGULAR,
+            pltpu.SemaphoreType.REGULAR((3,)),
         ]
         results = pl.pallas_call(
-            lambda *refs: kernel(strips, *refs),
+            lambda *refs: pl.run_scoped(
+                lambda in_sem: kernel(strips, refs, in_sem), pltpu.SemaphoreType.DMA((15,))
+            ),
             name="pyramid",
             out_shape=[
-                pltpu.VMEM((IMAGES, STRIP[k], COLS[k], CHANNELS), BF16) for k in (0, 2, 3)
+                pltpu.VMEM((1 if k == 0 else IMAGES, STRIP[k], COLS[k], CHANNELS), BF16)
+                for k in (0, 2, 3)
             ]
             + [
                 pltpu.VMEM((IMAGES, STRIP[1] * COLS[1], CHANNELS), F32),
                 pltpu.VMEM((1, 128), F32),
-                pltpu.VMEM((2, CHANNELS), F32),
+                pltpu.VMEM((4, CHANNELS), F32),
+                pltpu.VMEM((IMAGES, STRIP[0] * COLS[0], CHANNELS), F32),
             ],
             in_specs=[pl.BlockSpec(memory_space=pltpu.HBM)] * 12,
-            out_specs=[pl.BlockSpec(memory_space=pltpu.VMEM)] * 6,
+            out_specs=[pl.BlockSpec(memory_space=pltpu.VMEM)] * 7,
             scratch_shapes=scratch,
             compiler_params=pltpu.CompilerParams(
                 collective_id=0, has_side_effects=True, vmem_limit_bytes=48 << 20
@@ -587,12 +621,14 @@
                     jax.ShapeDtypeStruct((IMAGES, STRIP[k], COLS[k], CHANNELS), BF16)
                     for k in range(4)
                 ],
-                in_specs=[pl.BlockSpec(memory_space=pltpu.VMEM)] * 6,
+                in_specs=[pl.BlockSpec(memory_space=pltpu.VMEM)] * 7,
                 out_specs=[pl.BlockSpec(memory_space=pltpu.HBM)] * 4,
                 scratch_shapes=[
+                    pltpu.VMEM((STRIP[0], COLS[0], CHANNELS), BF16),
                     pltpu.VMEM((IMAGES, STRIP[1], COLS[1], CHANNELS), BF16),
-                    pltpu.SemaphoreType.DMA((4,)),
+                    pltpu.SemaphoreType.DMA((6,)),
                 ],
+                compiler_params=pltpu.CompilerParams(vmem_limit_bytes=8 << 20),
                 cost_estimate=pl.CostEstimate(
                     flops=0, bytes_accessed=5_600_000, transcendentals=0
                 ),

time: 26.8 us -> 25.9 us (0.966)
  Pallas kernels: 26.1 us -> 25.2 us
    pallas_call x1, Pallas kernels: 24.5 us -> 23.6 us  [per_device(): pl.pallas_call(lambda *refs: pl.run_scoped(lambda in_sem: kernel(strips,...]
where the time goes in v4:
time: 25.9 us; the launch traced here: 25.8 us
  Pallas kernels  25.2 us (97%)
  between operations  0.64 us (2%)
    pallas_call x1, Pallas kernels, per_device(): pl.pallas_call(lambda *refs: pl.run_scoped(lambda in_sem: kernel(strips,...  23.6 us
    pallas_call x1, Pallas kernels, per_device(): pl.pallas_call(lambda *refs: write_out(strips, *refs), name='write', out_...  1.59 us

profile of v4, /device:TPU:1, one launch (start us, length us, event | category | flops | bytes accessed | tf_op | source)
XLA Modules:
  0.0 25.8 jit_solution(7498886035262509112)
XLA Ops:
  0.6 23.6 %pyramid.1 = (bf16[1,8,256,256]{3,2,1,0:T(8,128)(2,1)S(1)}, bf16[2,2,64,256]{3,2,1,0:T(8,128)(2,1)S(1)}, bf16[2,1,32,256]{3,2,1,0:T(8,128)(2,1)S(1)}, f32[2,512,...) custom-call(bf16[2,8,256,256]{3,2,1,0:T(8,128)(2,1)} %refs_0_.1, ...), custom_call_target="tpu_custom_call" | custom-call | flops 7430000128 | bytes 13300000 | tf_op jit(solution)/shard_map/pyramid/pallas_call | solution.py:591
  24.2 1.6 %write.1 = (bf16[2,8,256,256]{3,2,1,0:T(8,128)(2,1)}, bf16[2,4,128,256]{3,2,1,0:T(8,128)(2,1)}, bf16[2,2,64,256]{3,2,1,0:T(8,128)(2,1)}, bf16[2,1,32,256]{3,2,1,0:T(8,128)(2,1)}) custom-call(bf16[1,8,256,256]{3,2,1,0:T(8,128)(2,1)S(1)} %get-tuple-element.11.refs_0_, bf16[2,2,64,256]{3,2,1,0:T(8,128)(2,1)S(1)} %get-tuple-element.12.refs_1_, ...), custom_call_target="tpu_custom_call" | custom-call | bytes 5600000 | tf_op jit(solution)/shard_map/write/pallas_call | solution.py:617

commit v5 on v4

--- a/solution.py
+++ b/solution.py
@@ -387,30 +387,41 @@
         cv2[image, row * 256 : row * 256 + 512, :] = values
         tally(0, image, values)
 
-    for stage in (halo_five, merge_four, merge_three):
+    def conv_five():
+        values = product(
+            [[xc5[:, tap, slab].reshape(64, 128) for slab in range(6)] for tap in range(3)], 3
+        )
+        cv5[...] = values
         for image in range(IMAGES):
-            stage(image)
+            tally(3, image, values[32 * image : 32 * image + 32])
+
+    def conv_four():
+        values = product(
+            [
+                [xc4[:, tap : tap + 2, slab].reshape(256, 128) for slab in range(6)]
+                for tap in range(3)
+            ],
+            2,
+        )
+        cv4[...] = values
+        for image in range(IMAGES):
+            tally(2, image, values[128 * image : 128 * image + 128])
+
+
+    for image in range(IMAGES):
+        halo_five(image)
+    for image in range(IMAGES):
+        merge_four(image)
+    conv_five()
+    for image in range(IMAGES):
+        merge_three(image)
+    conv_four()
     for image in range(IMAGES):
         merge_middle(image)
+    for image in range(IMAGES):
         for row in (2, 4):
             conv_two(image, row)
 
-    values = product(
-        [[xc5[:, tap, slab].reshape(64, 128) for slab in range(6)] for tap in range(3)], 3
-    )
-    cv5[...] = values
-    for image in range(IMAGES):
-        tally(3, image, values[32 * image : 32 * image + 32])
-    values = product(
-        [
-            [xc4[:, tap : tap + 2, slab].reshape(256, 128) for slab in range(6)]
-            for tap in range(3)
-        ],
-        2,
-    )
-    cv4[...] = values
-    for image in range(IMAGES):
-        tally(2, image, values[128 * image : 128 * image + 128])
 
     def conv_three(row, rows):
         for image in range(IMAGES):
@@ -439,12 +450,12 @@
         put_row(rb2, base + 2, xc2.at[image, 8], both[0:256] + cv2[image, 1792:2048, :])
         put_row(rb2, base + 3, xc2.at[image, 9], (both[256:512] + outside) * keep_bottom)
 
+    conv_three(1, 2)
     for image in range(IMAGES):
         merge_ends(image)
+    for image in range(IMAGES):
         for row in (0, 6):
             conv_two(image, row)
-
-    conv_three(1, 2)
 
     def everyone(source, target, which):
         far = lambda i: min(i, SIDE - i)
@@ -476,8 +487,20 @@
         copy.start()
 
     phase("conv3")
-    for row in (0, 3):
-        conv_three(row, 1)
+    for image in range(IMAGES):
+        values = product(
+            [
+                [
+                    jnp.concatenate([xc3[image, row + tap, slab] for row in (0, 3)], 0)
+                    for slab in range(6)
+                ]
+                for tap in range(3)
+            ],
+            1,
+        )
+        cv3[image, 0:128] = values[0:128]
+        cv3[image, 384:512] = values[128:256]
+        tally(1, image, values)
 
     phase("encodeB")
     sendB[...] = encode(stats.at[1])

time: 25.9 us -> 25.6 us (0.988)
  Pallas kernels: 25.2 us -> 24.9 us
    pallas_call x1, Pallas kernels: 23.6 us -> 23.3 us  [per_device(): pl.pallas_call(lambda *refs: pl.run_scoped(lambda in_sem: kernel(strips,...]
where the time goes in v5:
time: 25.6 us; the launch traced here: 25.5 us
  Pallas kernels  24.9 us (97%)
  between operations  0.64 us (2%)
    pallas_call x1, Pallas kernels, per_device(): pl.pallas_call(lambda *refs: pl.run_scoped(lambda in_sem: kernel(strips,...  23.3 us
    pallas_call x1, Pallas kernels, per_device(): pl.pallas_call(lambda *refs: write_out(strips, *refs), name='write', out_...  1.59 us

profile of v5, /device:TPU:1, one launch (start us, length us, event | category | flops | bytes accessed | tf_op | source)
XLA Modules:
  0.0 25.5 jit_solution(3608963955151908009)
XLA Ops:
  0.6 23.3 %pyramid.1 = (bf16[1,8,256,256]{3,2,1,0:T(8,128)(2,1)S(1)}, bf16[2,2,64,256]{3,2,1,0:T(8,128)(2,1)S(1)}, bf16[2,1,32,256]{3,2,1,0:T(8,128)(2,1)S(1)}, f32[2,512,...) custom-call(bf16[2,8,256,256]{3,2,1,0:T(8,128)(2,1)} %refs_0_.1, ...), custom_call_target="tpu_custom_call" | custom-call | flops 7430000128 | bytes 13300000 | tf_op jit(solution)/shard_map/pyramid/pallas_call | solution.py:614
  23.9 1.6 %write.1 = (bf16[2,8,256,256]{3,2,1,0:T(8,128)(2,1)}, bf16[2,4,128,256]{3,2,1,0:T(8,128)(2,1)}, bf16[2,2,64,256]{3,2,1,0:T(8,128)(2,1)}, bf16[2,1,32,256]{3,2,1,0:T(8,128)(2,1)}) custom-call(bf16[1,8,256,256]{3,2,1,0:T(8,128)(2,1)S(1)} %get-tuple-element.11.refs_0_, bf16[2,2,64,256]{3,2,1,0:T(8,128)(2,1)S(1)} %get-tuple-element.12.refs_1_, ...), custom_call_target="tpu_custom_call" | custom-call | bytes 5600000 | tf_op jit(solution)/shard_map/write/pallas_call | solution.py:640

commit v6 on v5

--- a/solution.py
+++ b/solution.py
@@ -84,7 +84,7 @@
     return (values * factor + offset).astype(BF16)
 
 
-def kernel(strips, refs, in_sem):
+def kernel(strips, refs, in_sem, edge_send, edge_recv, all_send, all_recv, entered):
     (f2, f3, f4, f5, w2, w3, w4, w5, bias, smooth, gain, shift) = refs[:12]
     outs = {0: refs[12], 2: refs[13], 3: refs[14], 4: refs[16]}
     cv3 = refs[15]
@@ -101,7 +101,6 @@
         cv4, cv5,
         stats,
         sendA, sendB, recvA, recvB,
-        edge_send, edge_recv, all_send, all_recv, entered,
     ) = refs[19:]
     current = []
 
@@ -607,13 +606,16 @@
             vmem((4, 2, 2, 8, 256), F32),
             vmem((4, 128), F32), vmem((1, 128), F32),
             vmem((strips - 1, 4, 128), F32), vmem((strips - 1, 1, 128), F32),
-            pltpu.SemaphoreType.DMA((4, 2)), pltpu.SemaphoreType.DMA((4, 2)),
-            pltpu.SemaphoreType.DMA((2,)), pltpu.SemaphoreType.DMA((2,)),
-            pltpu.SemaphoreType.REGULAR((3,)),
         ]
         results = pl.pallas_call(
             lambda *refs: pl.run_scoped(
-                lambda in_sem: kernel(strips, refs, in_sem), pltpu.SemaphoreType.DMA((15,))
+                lambda *semaphores: kernel(strips, refs, *semaphores),
+                pltpu.SemaphoreType.DMA((15,)),
+                pltpu.SemaphoreType.DMA((4, 2)),
+                pltpu.SemaphoreType.DMA((4, 2)),
+                pltpu.SemaphoreType.DMA((2,)),
+                pltpu.SemaphoreType.DMA((2,)),
+                pltpu.SemaphoreType.REGULAR((3,)),
             ),
             name="pyramid",
             out_shape=[
@@ -638,7 +640,9 @@
         )(*(pltpu.with_memory_space_constraint(a, pltpu.HBM) for a in args))
         return tuple(
             pl.pallas_call(
-                lambda *refs: write_out(strips, *refs),
+                lambda *refs: pl.run_scoped(
+                    lambda sems: write_out(strips, *refs, sems), pltpu.SemaphoreType.DMA((6,))
+                ),
                 name="write",
                 out_shape=[
                     jax.ShapeDtypeStruct((IMAGES, STRIP[k], COLS[k], CHANNELS), BF16)
@@ -649,7 +653,6 @@
                 scratch_shapes=[
                     pltpu.VMEM((STRIP[0], COLS[0], CHANNELS), BF16),
                     pltpu.VMEM((IMAGES, STRIP[1], COLS[1], CHANNELS), BF16),
-                    pltpu.SemaphoreType.DMA((6,)),
                 ],
                 compiler_params=pltpu.CompilerParams(vmem_limit_bytes=8 << 20),
                 cost_estimate=pl.CostEstimate(

time: 25.6 us -> 25.3 us (0.988)
  Pallas kernels: 24.9 us -> 24.6 us
    pallas_call x2, Pallas kernels: 24.9 us -> 24.6 us  [the longest x1 23.1 us: per_device(): pl.pallas_call(lambda *refs: pl.run_scoped(lambda *semaphores: kernel(str...]
where the time goes in v6:
time: 25.3 us; the launch traced here: 25.2 us
  Pallas kernels  24.6 us (97%)
  between operations  0.64 us (3%)
    pallas_call x1, Pallas kernels, per_device(): pl.pallas_call(lambda *refs: pl.run_scoped(lambda *semaphores: kernel(str...  23.1 us
    pallas_call x1, Pallas kernels, per_device(): pl.pallas_call(lambda *refs: pl.run_scoped(lambda sems: write_out(strips,...  1.54 us

profile of v6, /device:TPU:1, one launch (start us, length us, event | category | flops | bytes accessed | tf_op | source)
XLA Modules:
  0.0 25.2 jit_solution(7138217667022115899)
XLA Ops:
  0.6 23.1 %pyramid.1 = (bf16[1,8,256,256]{3,2,1,0:T(8,128)(2,1)S(1)}, bf16[2,2,64,256]{3,2,1,0:T(8,128)(2,1)S(1)}, bf16[2,1,32,256]{3,2,1,0:T(8,128)(2,1)S(1)}, f32[2,512,...) custom-call(bf16[2,8,256,256]{3,2,1,0:T(8,128)(2,1)} %refs_0_.1, ...), custom_call_target="tpu_custom_call" | custom-call | flops 7430000128 | bytes 13300000 | tf_op jit(solution)/shard_map/pyramid/pallas_call | solution.py:610
  23.7 1.5 %write.1 = (bf16[2,8,256,256]{3,2,1,0:T(8,128)(2,1)}, bf16[2,4,128,256]{3,2,1,0:T(8,128)(2,1)}, bf16[2,2,64,256]{3,2,1,0:T(8,128)(2,1)}, bf16[2,1,32,256]{3,2,1,0:T(8,128)(2,1)}) custom-call(bf16[1,8,256,256]{3,2,1,0:T(8,128)(2,1)S(1)} %get-tuple-element.11.refs_0_, bf16[2,2,64,256]{3,2,1,0:T(8,128)(2,1)S(1)} %get-tuple-element.12.refs_1_, ...), custom_call_target="tpu_custom_call" | custom-call | bytes 5600000 | tf_op jit(solution)/shard_map/write/pallas_call | solution.py:642

commit v7 on v6

--- a/solution.py
+++ b/solution.py
@@ -395,17 +395,10 @@
             tally(3, image, values[32 * image : 32 * image + 32])
 
     def conv_four():
-        values = product(
-            [
-                [xc4[:, tap : tap + 2, slab].reshape(256, 128) for slab in range(6)]
-                for tap in range(3)
-            ],
-            2,
-        )
-        cv4[...] = values
         for image in range(IMAGES):
-            tally(2, image, values[128 * image : 128 * image + 128])
-
+            values = conv(xc4, 2, image, 0, 2)
+            cv4[128 * image : 128 * image + 128] = values
+            tally(2, image, values)
 
     for image in range(IMAGES):
         halo_five(image)

time: 25.3 us -> 25.2 us (level)
  no operation moved by 1% of the time
where the time goes in v7:
time: 25.2 us; the launch traced here: 25.1 us
  Pallas kernels  24.5 us (97%)
  between operations  0.64 us (3%)
    pallas_call x1, Pallas kernels, per_device(): pl.pallas_call(lambda *refs: pl.run_scoped(lambda *semaphores: kernel(str...  22.9 us
    pallas_call x1, Pallas kernels, per_device(): pl.pallas_call(lambda *refs: pl.run_scoped(lambda sems: write_out(strips,...  1.54 us

profile of v7, /device:TPU:1, one launch (start us, length us, event | category | flops | bytes accessed | tf_op | source)
XLA Modules:
  0.0 25.1 jit_solution(16488265028852692443)
XLA Ops:
  0.6 22.9 %pyramid.1 = (bf16[1,8,256,256]{3,2,1,0:T(8,128)(2,1)S(1)}, bf16[2,2,64,256]{3,2,1,0:T(8,128)(2,1)S(1)}, bf16[2,1,32,256]{3,2,1,0:T(8,128)(2,1)S(1)}, f32[2,512,...) custom-call(bf16[2,8,256,256]{3,2,1,0:T(8,128)(2,1)} %refs_0_.1, ...), custom_call_target="tpu_custom_call" | custom-call | flops 7430000128 | bytes 13300000 | tf_op jit(solution)/shard_map/pyramid/pallas_call | solution.py:603
  23.6 1.5 %write.1 = (bf16[2,8,256,256]{3,2,1,0:T(8,128)(2,1)}, bf16[2,4,128,256]{3,2,1,0:T(8,128)(2,1)}, bf16[2,2,64,256]{3,2,1,0:T(8,128)(2,1)}, bf16[2,1,32,256]{3,2,1,0:T(8,128)(2,1)}) custom-call(bf16[1,8,256,256]{3,2,1,0:T(8,128)(2,1)S(1)} %get-tuple-element.11.refs_0_, bf16[2,2,64,256]{3,2,1,0:T(8,128)(2,1)S(1)} %get-tuple-element.12.refs_1_, ...), custom_call_target="tpu_custom_call" | custom-call | bytes 5600000 | tf_op jit(solution)/shard_map/write/pallas_call | solution.py:635
